TPU v7x, 32 devices: a whole 2x2x4 slice. The times are simulated.
32 devices in a mesh: row: 4 (over x, core), col: 4 (over z), depth: 2 (over y).
Axes of the slice: x: 2, y: 2, z: 4, core: 2. Of those that a mesh axis runs over, the one named last changes fastest.
Arguments:
- tokens: bfloat16 [512, 4096], P(('col', 'depth'), 'row'), may hold values from -6 to 6
- w_gate: bfloat16 [4096, 14336], P('row', 'col'), may hold values from -0.09375 to 0.09375
- w_up: bfloat16 [4096, 14336], P('row', 'col'), may hold values from -0.09375 to 0.09375
- w_down: bfloat16 [14336, 4096], P('col', 'row'), may hold values from -0.046875 to 0.046875
- cotangent: bfloat16 [512, 4096], P(('col', 'depth'), 'row'), may hold values from -0.25 to 0.25
Outputs:
- mixed: bfloat16 [512, 4096], P(('col', 'depth'), 'row')
- grad_gate: bfloat16 [4096, 14336], P(('row', 'depth'), 'col')
- grad_up: bfloat16 [4096, 14336], P(('row', 'depth'), 'col')
- grad_down: bfloat16 [14336, 4096], P(('col', 'depth'), 'row')
All inputs are finite; a program needn't handle non-finite values.
Results may differ from a plain program's by a relative error of at most 0.025.
Values may be sent and summed in bfloat16 or wider, within the bound.
A program may use at most 128 MiB of HBM per device.

v0:
```python
import functools

import jax
import jax.numpy as jnp
from jax import lax
from jax.experimental import pallas as pl
from jax.experimental.pallas import tpu as pltpu
from jax.sharding import PartitionSpec as P

COLS_CONTRACT = (((1,), (1,)), ((), ()))
ROWS_CONTRACT = (((0,), (0,)), ((), ()))


def gate_grads(hidden_grad, gate_sum, up_sum):
    sigmoid_gate = jax.nn.sigmoid(gate_sum)
    d_gate = (hidden_grad * up_sum * sigmoid_gate * (1.0 + gate_sum * (1.0 - sigmoid_gate))).astype(
        jnp.bfloat16
    )
    d_up = (hidden_grad * gate_sum * sigmoid_gate).astype(jnp.bfloat16)
    return (d_gate, d_up)


def layered_device(tokens, w_gate, w_up, w_down, cotangent):
    hid_width = w_gate.shape[1]
    token_rows = lax.all_gather(tokens, "col", axis=0, tiled=True)
    row_piece = token_rows
    joined = lax.psum_scatter(
        jnp.concatenate(
            [
                jnp.dot(row_piece, w_gate, preferred_element_type=jnp.float32),
                jnp.dot(row_piece, w_up, preferred_element_type=jnp.float32),
            ],
            axis=1,
        ).astype(jnp.bfloat16),
        "row",
        scatter_dimension=0,
        tiled=True,
    ).astype(jnp.float32)
    gate_sum = joined[:, :hid_width]
    up_sum = joined[:, hid_width:]
    hidden = (jax.nn.silu(gate_sum) * up_sum).astype(jnp.bfloat16)
    hidden_rows = lax.all_gather(hidden, "row", axis=0, tiled=True)
    row_piece = hidden_rows
    mixed = lax.psum_scatter(
        jnp.dot(row_piece, w_down, preferred_element_type=jnp.float32).astype(jnp.bfloat16),
        "col",
        scatter_dimension=0,
        tiled=True,
    )
    cot_rows = lax.all_gather(cotangent, "col", axis=0, tiled=True)
    row_piece = cot_rows
    hidden_grad = lax.psum_scatter(
        lax.dot_general(
            row_piece, w_down, COLS_CONTRACT, preferred_element_type=jnp.float32
        ).astype(jnp.bfloat16),
        "row",
        scatter_dimension=0,
        tiled=True,
    ).astype(jnp.float32)
    d_gate, d_up = gate_grads(hidden_grad, gate_sum, up_sum)
    d_gate_rows, d_up_rows = (
        lax.all_gather(d_gate, "row", axis=0, tiled=True),
        lax.all_gather(d_up, "row", axis=0, tiled=True),
    )
    down_term = lax.dot_general(
        hidden_rows, cot_rows, ROWS_CONTRACT, preferred_element_type=jnp.float32
    )
    grad_down = lax.psum_scatter(
        down_term.astype(jnp.bfloat16), "depth", scatter_dimension=0, tiled=True
    )
    layer_tokens = lax.all_to_all(token_rows, "depth", split_axis=1, concat_axis=0, tiled=True)
    block_rows = token_rows.shape[0]
    empty_grad = jnp.zeros((layer_tokens.shape[1], d_gate_rows.shape[1]), jnp.float32)
    first_row = jnp.int32(0)
    gate_total = empty_grad
    up_total = empty_grad
    gate_piece = lax.all_gather(d_gate_rows, "depth", axis=0, tiled=True)
    up_piece = lax.all_gather(d_up_rows, "depth", axis=0, tiled=True)
    for sub_index in range(gate_piece.shape[0] // block_rows):
        gate_block = gate_piece[sub_index * block_rows : (sub_index + 1) * block_rows]
        up_block = up_piece[sub_index * block_rows : (sub_index + 1) * block_rows]
        offset = first_row + sub_index * block_rows
        tok_block = lax.dynamic_slice_in_dim(layer_tokens, offset, block_rows, 0)
        gate_part = lax.optimization_barrier(
            lax.dot_general(
                tok_block, gate_block, ROWS_CONTRACT, preferred_element_type=jnp.float32
            ).astype(jnp.bfloat16)
        )
        up_part = lax.optimization_barrier(
            lax.dot_general(
                tok_block, up_block, ROWS_CONTRACT, preferred_element_type=jnp.float32
            ).astype(jnp.bfloat16)
        )
        gate_total = gate_total + gate_part.astype(jnp.float32)
        up_total = up_total + up_part.astype(jnp.float32)
    return (mixed, gate_total.astype(jnp.bfloat16), up_total.astype(jnp.bfloat16), grad_down)


MESH = pl.DeviceIdType.MESH
VMEM_LIMIT = 66_000_000


def f32(x):
    return x.astype(jnp.float32)


def bf16(x):
    return x.astype(jnp.bfloat16)


def rows_dot(x, y):
    return lax.dot_general(x, y, ROWS_CONTRACT, preferred_element_type=jnp.float32)


def exchange_kernel(
    n_row,
    n_col,
    tok_in,
    gate_in,
    up_in,
    down_in,
    cot_in,
    mixed_out,
    tok_out,
    cot_out,
    hid_out,
    dgate_out,
    dup_out,
    tok_v,
    cot_v,
    tok_far,
    cot_far,
    gate_v,
    up_v,
    down_v,
    core_send_v,
    core_recv_v,
    own_v,
    x_send_v,
    x_recv_v,
    near_v,
    far_v,
    far_hid_v,
    mix_own_v,
    mix_send_v,
    mix_recv_v,
    load_tok_sem,
    load_w_sem,
    z_send,
    z_recv,
    yt_send,
    yt_recv,
    core_send,
    core_recv,
    x_send,
    x_recv,
    near_send,
    near_recv,
    y_send,
    y_recv,
    yh_send,
    yh_recv,
    fwd_send,
    fwd_recv,
    fwdh_send,
    fwdh_recv,
    mix_send,
    mix_recv,
    out_sem,
):
    row, col, layer = lax.axis_index("row"), lax.axis_index("col"), lax.axis_index("depth")
    core = row % 2
    other = 1 - core
    far_layer = 1 - layer
    blocks, rows, feats = tok_v.shape
    half_feats = tok_far.shape[2]
    quarter = gate_v.shape[2]
    units = x_send_v.shape[0]

    core_id = (row + 1 - 2 * core, col, layer)
    x_id = ((row + 2) % n_row, col, layer)
    y_id = (row, col, far_layer)
    z_ids = {
        1: (row, n_col - 1 - col, layer),
        2: (row, (col + 2) % n_col, layer),
        3: (row, col + 1 - 2 * (col % 2), layer),
    }

    def remote(src, dst, send, recv, device):
        return pltpu.make_async_remote_copy(
            src_ref=src, dst_ref=dst, send_sem=send, recv_sem=recv, device_id=device, device_id_type=MESH
        )

    def load_weight(array, part):
        source = (gate_in, up_in, down_in)[array]
        target = (gate_v, up_v, down_v)[array]
        span = slice(part * quarter, (part + 1) * quarter)
        view = source.at[span, :] if array == 2 else source.at[:, span]
        return pltpu.make_async_copy(view, target.at[part], load_w_sem.at[array, part])

    load_tok = pltpu.make_async_copy(tok_in, tok_v.at[0], load_tok_sem.at[0])
    load_cot = pltpu.make_async_copy(cot_in, cot_v.at[0], load_tok_sem.at[1])
    load_tok.start()
    load_cot.start()
    for pair in range(2):
        for array in range(3):
            for part in (2 * pair, 2 * pair + 1):
                load_weight(array, part).start()

    barrier = pltpu.get_barrier_semaphore()
    peers = [core_id, x_id, y_id] + [z_ids[b] for b in range(1, blocks)]
    for peer in peers:
        pl.semaphore_signal(barrier, inc=1, device_id=peer, device_id_type=MESH)
    pl.semaphore_wait(barrier, len(peers))

    def z_copy(array, b):
        buffer = (tok_v, cot_v)[array]
        return remote(buffer.at[0], buffer.at[b], z_send.at[array, b], z_recv.at[array, b], z_ids[b])

    load_tok.wait()
    for b in range(1, blocks):
        z_copy(0, b).start()
    load_cot.wait()
    for b in range(1, blocks):
        z_copy(1, b).start()

    def yt_copy(b, array):
        if array == 0:
            lanes = pl.ds(pl.multiple_of(far_layer * half_feats, 128), half_feats)
            return remote(tok_v.at[b, :, lanes], tok_far.at[b], yt_send.at[b, 0], yt_recv.at[b, 0], y_id)
        return remote(cot_v.at[b], cot_far.at[b], yt_send.at[b, 1], yt_recv.at[b, 1], y_id)

    def out_rows(b, far):
        return pl.ds(pl.multiple_of((b + far * blocks) * rows, rows), rows)

    def send_out(src, dst, slot):
        pltpu.make_async_copy(src, dst, out_sem.at[slot]).start()

    def core_copy(u, a):
        return remote(
            core_send_v.at[u, a], core_recv_v.at[u, a], core_send.at[u, a], core_recv.at[u, a], core_id
        )

    def x_copy(u, a):
        return remote(x_send_v.at[u, a], x_recv_v.at[u, a], x_send.at[u, a], x_recv.at[u, a], x_id)

    def near_copy(u):
        return remote(near_v.at[core, u], near_v.at[core, u], near_send.at[u], near_recv.at[u], core_id)

    def near_arrival(u):
        return remote(near_v.at[other, u], near_v.at[other, u], near_send.at[u], near_recv.at[u], core_id)

    def y_copy(u):
        return remote(near_v.at[core, u, 0:2], far_v.at[core, u], y_send.at[u], y_recv.at[u], y_id)

    def yh_copy(u, b):
        return remote(near_v.at[core, u, 2], far_hid_v.at[core, b], yh_send.at[b], yh_recv.at[b], y_id)

    def fwd_copy(u):
        return remote(far_v.at[core, u], far_v.at[core, u], fwd_send.at[u], fwd_recv.at[u], core_id)

    def fwd_arrival(u):
        return remote(far_v.at[other, u], far_v.at[other, u], fwd_send.at[u], fwd_recv.at[u], core_id)

    def fwdh_copy(b):
        return remote(far_hid_v.at[core, b], far_hid_v.at[core, b], fwdh_send.at[b], fwdh_recv.at[b], core_id)

    def fwdh_arrival(b):
        return remote(
            far_hid_v.at[other, b], far_hid_v.at[other, b], fwdh_send.at[b], fwdh_recv.at[b], core_id
        )

    def mix_copy(b):
        return remote(mix_send_v.at[b], mix_recv_v.at[b], mix_send.at[b], mix_recv.at[b], z_ids[b])

    def grads_out(pair, u, side, far):
        q, b = u % 2, u // 2
        lanes = pl.ds(pl.multiple_of((2 * q + side) * quarter, 128), quarter)
        send_out(pair[0], dgate_out.at[out_rows(b, far), lanes], 3)
        send_out(pair[1], dup_out.at[out_rows(b, far), lanes], 4)

    def hid_to_out(src, b, side, far):
        lanes = pl.ds(pl.multiple_of(side * quarter, 128), quarter)
        send_out(src, hid_out.at[out_rows(b, far), lanes], 2)

    def products(u, array):
        q, b = u % 2, u // 2
        for side, keep in ((other, False), (core, True)):
            part = 2 * q + side
            if array == 2:
                value = lax.dot_general(
                    cot_v[b], down_v[part], COLS_CONTRACT, preferred_element_type=jnp.float32
                )
            else:
                weight = (gate_v, up_v)[array]
                value = jnp.dot(tok_v[b], weight[part], preferred_element_type=jnp.float32)
            if keep:
                own_v[u, array] = value
            else:
                core_send_v[u, array] = bf16(value)
                core_copy(u, array).start()

    def finish(u, array):
        core_copy(u, array).wait_recv()
        total = own_v[u, array] + f32(core_recv_v[u, array])
        own_v[u, array] = total
        x_send_v[u, array] = bf16(total)
        x_copy(u, array).start()

    def wait_weight(u, array):
        q = u % 2
        for pair in range(2):

            @pl.when((u < 2) & (q == pair))
            def _():
                load_weight(array, 2 * pair).wait()
                load_weight(array, 2 * pair + 1).wait()

    def compute_unit(u):
        q, b = u % 2, u // 2

        for static_b in range(1, blocks):

            @pl.when((b == static_b) & (q == 0))
            def _():
                z_copy(0, static_b).wait_recv()
                z_copy(1, static_b).wait_recv()

        @pl.when(q == 0)
        def _():
            own_lanes = pl.ds(pl.multiple_of(layer * half_feats, 128), half_feats)
            yt_copy(b, 0).start()
            yt_copy(b, 1).start()
            send_out(tok_v.at[b, :, own_lanes], tok_out.at[out_rows(b, 0), :], 0)
            send_out(cot_v.at[b], cot_out.at[out_rows(b, 0), :], 1)

        wait_weight(u, 0)
        products(u, 0)
        wait_weight(u, 1)
        products(u, 1)
        finish(u, 0)
        wait_weight(u, 2)
        products(u, 2)
        finish(u, 1)
        finish(u, 2)

    row_step = 16

    def combine(u):
        q, b = u % 2, u // 2
        for a in range(3):
            x_copy(u, a).wait_recv()

        def some_rows(i, carry):
            span = pl.ds(pl.multiple_of(i * row_step, row_step), row_step)
            gate_sum = own_v[u, 0, span, :] + f32(x_recv_v[u, 0, span, :])
            up_sum = own_v[u, 1, span, :] + f32(x_recv_v[u, 1, span, :])
            hidden_grad = own_v[u, 2, span, :] + f32(x_recv_v[u, 2, span, :])
            sigmoid_gate = jax.nn.sigmoid(gate_sum)
            swish = gate_sum * sigmoid_gate
            near_v[core, u, 2, span, :] = bf16(swish * up_sum)
            near_v[core, u, 1, span, :] = bf16(hidden_grad * swish)
            near_v[core, u, 0, span, :] = bf16(
                hidden_grad * up_sum * sigmoid_gate * (1.0 + gate_sum * (1.0 - sigmoid_gate))
            )
            return carry

        lax.fori_loop(0, rows // row_step, some_rows, 0)
        near_copy(u).start()
        y_copy(u).start()

        @pl.when(q == far_layer)
        def _():
            yh_copy(u, b).start()

        grads_out((near_v.at[core, u, 0], near_v.at[core, u, 1]), u, core, 0)

        @pl.when(q == layer)
        def _():
            hid_to_out(near_v.at[core, u, 2], b, core, 0)

    def near_arrived(u):
        q, b = u % 2, u // 2
        near_arrival(u).wait_recv()
        grads_out((near_v.at[other, u, 0], near_v.at[other, u, 1]), u, other, 0)

        @pl.when(q == layer)
        def _():
            hid_to_out(near_v.at[other, u, 2], b, other, 0)

        @pl.when(q == 1)
        def _():
            total = jnp.zeros((rows, feats), jnp.float32)
            for half in range(2):
                for side in range(2):
                    total = total + jnp.dot(
                        near_v[side, 2 * b + half, 2],
                        down_v[2 * half + side],
                        preferred_element_type=jnp.float32,
                    )

            @pl.when(b == 0)
            def _():
                mix_own_v[...] = total

            @pl.when(b > 0)
            def _():
                mix_send_v[b] = bf16(total)

            for static_b in range(1, blocks):

                @pl.when(b == static_b)
                def _():
                    mix_copy(static_b).start()

    def far_arrived(u):
        q, b = u % 2, u // 2
        y_copy(u).wait_recv()
        fwd_copy(u).start()
        grads_out((far_v.at[core, u, 0], far_v.at[core, u, 1]), u, core, 1)

        @pl.when(q == layer)
        def _():
            yh_copy(u, b).wait_recv()
            fwdh_copy(b).start()
            hid_to_out(far_hid_v.at[core, b], b, core, 1)

        @pl.when(q == 0)
        def _():
            yt_copy(b, 0).wait_recv()
            yt_copy(b, 1).wait_recv()
            send_out(tok_far.at[b], tok_out.at[out_rows(b, 1), :], 0)
            send_out(cot_far.at[b], cot_out.at[out_rows(b, 1), :], 1)

    def forwarded(u):
        q, b = u % 2, u // 2
        fwd_arrival(u).wait_recv()
        grads_out((far_v.at[other, u, 0], far_v.at[other, u, 1]), u, other, 1)

        @pl.when(q == layer)
        def _():
            fwdh_arrival(b).wait_recv()
            hid_to_out(far_hid_v.at[other, b], b, other, 1)

    stages = ((compute_unit, 0), (combine, 2), (near_arrived, 3), (far_arrived, 4), (forwarded, 5))

    def step(s, carry):
        for stage, lag in stages:

            @pl.when((s >= lag) & (s < units + lag))
            def _():
                stage(s - lag)

        return carry

    lax.fori_loop(0, units + stages[-1][1], step, 0)

    total = mix_own_v[...]
    for b in range(1, blocks):
        mix_copy(b).wait_recv()
        total = total + f32(mix_recv_v[b])
    mixed_out[...] = bf16(total)

    for b in range(1, blocks):
        z_copy(0, b).wait_send()
        z_copy(1, b).wait_send()
        mix_copy(b).wait_send()

    def drain_block(b, carry):
        yt_copy(b, 0).wait_send()
        yt_copy(b, 1).wait_send()
        yh_copy(2 * b, b).wait_send()
        fwdh_copy(b).wait_send()
        return carry

    def drain_unit(u, carry):
        for a in range(3):
            core_copy(u, a).wait_send()
            x_copy(u, a).wait_send()
        near_copy(u).wait_send()
        y_copy(u).wait_send()
        fwd_copy(u).wait_send()
        return carry

    lax.fori_loop(0, blocks, drain_block, 0)
    lax.fori_loop(0, units, drain_unit, 0)
    for slot, out in enumerate((tok_out, cot_out, hid_out, dgate_out, dup_out)):
        pltpu.make_async_copy(out, out, out_sem.at[slot]).wait()


def grid_device(n_row, n_col, tokens, w_gate, w_up, w_down, cotangent):
    rows, feats = tokens.shape
    hid = w_gate.shape[1]
    quarter = hid // 4
    blocks = n_col
    units = 2 * blocks
    all_rows = 2 * blocks * rows
    narrow, wide = jnp.bfloat16, jnp.float32
    dma = pltpu.SemaphoreType.DMA
    scratch = [
        pltpu.VMEM((blocks, rows, feats), narrow),
        pltpu.VMEM((blocks, rows, feats), narrow),
        pltpu.VMEM((blocks, rows, feats // 2), narrow),
        pltpu.VMEM((blocks, rows, feats), narrow),
        pltpu.VMEM((4, feats, quarter), narrow),
        pltpu.VMEM((4, feats, quarter), narrow),
        pltpu.VMEM((4, quarter, feats), narrow),
        pltpu.VMEM((units, 3, rows, quarter), narrow),
        pltpu.VMEM((units, 3, rows, quarter), narrow),
        pltpu.VMEM((units, 3, rows, quarter), wide),
        pltpu.VMEM((units, 3, rows, quarter), narrow),
        pltpu.VMEM((units, 3, rows, quarter), narrow),
        pltpu.VMEM((2, units, 3, rows, quarter), narrow),
        pltpu.VMEM((2, units, 2, rows, quarter), narrow),
        pltpu.VMEM((2, blocks, rows, quarter), narrow),
        pltpu.VMEM((rows, feats), wide),
        pltpu.VMEM((blocks, rows, feats), narrow),
        pltpu.VMEM((blocks, rows, feats), narrow),
        dma((2,)),
        dma((3, 4)),
        dma((2, blocks)),
        dma((2, blocks)),
        dma((blocks, 2)),
        dma((blocks, 2)),
        dma((units, 3)),
        dma((units, 3)),
        dma((units, 3)),
        dma((units, 3)),
        dma((units,)),
        dma((units,)),
        dma((units,)),
        dma((units,)),
        dma((blocks,)),
        dma((blocks,)),
        dma((units,)),
        dma((units,)),
        dma((blocks,)),
        dma((blocks,)),
        dma((blocks,)),
        dma((blocks,)),
        dma((5,)),
    ]
    mixed, tok, cot, hidden, d_gate, d_up = pl.pallas_call(
        functools.partial(exchange_kernel, n_row, n_col),
        out_shape=[
            jax.ShapeDtypeStruct((rows, feats), narrow),
            jax.ShapeDtypeStruct((all_rows, feats // 2), narrow),
            jax.ShapeDtypeStruct((all_rows, feats), narrow),
            jax.ShapeDtypeStruct((all_rows, hid // 2), narrow),
            jax.ShapeDtypeStruct((all_rows, hid), narrow),
            jax.ShapeDtypeStruct((all_rows, hid), narrow),
        ],
        in_specs=[pl.BlockSpec(memory_space=pl.ANY)] * 5,
        out_specs=[pl.BlockSpec(memory_space=pltpu.VMEM)] + [pl.BlockSpec(memory_space=pl.ANY)] * 5,
        scratch_shapes=scratch,
        compiler_params=pltpu.CompilerParams(
            collective_id=0, has_side_effects=True, vmem_limit_bytes=VMEM_LIMIT
        ),
    )(tokens, w_gate, w_up, w_down, cotangent)
    grad_gate = bf16(rows_dot(tok, d_gate))
    grad_up = bf16(rows_dot(tok, d_up))
    grad_down = bf16(rows_dot(hidden, cot))
    return (mixed, grad_gate, grad_up, grad_down)


def solution(mesh):
    placed = (
        P(("col", "depth"), "row"),
        P("row", "col"),
        P("row", "col"),
        P("col", "row"),
        P(("col", "depth"), "row"),
    )
    n_row, n_col = mesh.shape["row"], mesh.shape["col"]
    if (n_row, n_col, mesh.shape["depth"]) == (4, 4, 2):
        per_device = functools.partial(grid_device, n_row, n_col)
    else:
        per_device = layered_device
    return jax.shard_map(
        per_device,
        mesh=mesh,
        in_specs=placed,
        out_specs=(
            P(("col", "depth"), "row"),
            P(("row", "depth"), "col"),
            P(("row", "depth"), "col"),
            P(("col", "depth"), "row"),
        ),
        check_vma=False,
    )
```

profile of v0, /device:TPU:9, one launch (start us, length us, event | category | flops | bytes accessed | tf_op | source)
XLA Modules:
  0.0 113.7 jit_solution(1467259247641621669)
XLA Ops:
  0.6 98.2 %shard_map.84 = (bf16[64,1024]{1,0:T(8,128)(2,1)}, bf16[512,512]{1,0:T(8,128)(2,1)}, bf16[512,1024]{1,0:T(8,128)(2,1)}, bf16[512,1792]{1,0:T(8,128)(2,1)}, bf16[...) custom-call(bf16[64,1024]{1,0:T(8,128)(2,1)} %tok_in.1, bf16[1024,3584]{1,0:T(8,128)(2,1)} %gate_in.1, ...), custom_call_target="tpu_custom_call" | custom-call | tf_op jit(solution)/shard_map/pallas_call | solution.py:543
  98.8 0.0 copy-start
  98.8 0.0 copy-start.1
  98.8 6.3 %convolution_convert_fusion.1 = bf16[512,3584]{1,0:T(8,128)(2,1)} fusion(bf16[512,512]{1,0:T(8,128)(2,1)} %get-tuple-element.11, bf16[512,3584]{1,0:T(8,128)(2,1)} %get-tuple-element.12), kind=kOutput, calls=%fused_computation.1 | convolution fusion | flops 1880883200 | bytes 7864320 | tf_op jit(solution)/shard_map/dot_general | solution.py:112
  105.1 0.0 copy-done
  105.1 0.0 copy-done.1
  105.1 0.0 copy-start.3
  105.1 0.0 copy-start.4
  105.1 3.9 %convolution_convert_fusion = bf16[512,3584]{1,0:T(8,128)(2,1)} fusion(bf16[512,512]{1,0:T(8,128)(2,1)S(1)} %copy-done.1, bf16[512,3584]{1,0:T(8,128)(2,1)S(1)} %copy-done), kind=kOutput, calls=%fused_computation | convolution fusion | flops 1880883200 | bytes 7864320 | tf_op jit(solution)/shard_map/dot_general | solution.py:112
  109.1 0.0 copy-done.3
  109.1 0.0 copy-done.4
  109.1 0.0 copy-start.2
  109.1 3.9 %convolution_convert_fusion.2 = bf16[1792,1024]{1,0:T(8,128)(2,1)} fusion(bf16[512,1792]{1,0:T(8,128)(2,1)S(1)} %copy-done.3, bf16[512,1024]{1,0:T(8,128)(2,1)S(1)} %copy-done.4), kind=kOutput, calls=%fused_computation.2 | convolution fusion | flops 1880883200 | bytes 6553600 | tf_op jit(solution)/shard_map/dot_general | solution.py:112
  113.0 0.0 copy-done.2
  113.0 0.7 copy.10
Async XLA Ops:
  98.8 6.3 %copy-start = (bf16[512,3584]{1,0:T(8,128)(2,1)S(1)}, bf16[512,3584]{1,0:T(8,128)(2,1)}, u32[]{:S(2)}) copy-start(bf16[512,3584]{1,0:T(8,128)(2,1)} %get-tuple-element.13) | copy-start | bytes 11010052
  98.8 6.3 %copy-start.1 = (bf16[512,512]{1,0:T(8,128)(2,1)S(1)}, bf16[512,512]{1,0:T(8,128)(2,1)}, u32[]{:S(2)}) copy-start(bf16[512,512]{1,0:T(8,128)(2,1)} %get-tuple-element.11) | copy-start | bytes 1572868
  105.1 4.0 %copy-start.3 = (bf16[512,1792]{1,0:T(8,128)(2,1)S(1)}, bf16[512,1792]{1,0:T(8,128)(2,1)}, u32[]{:S(2)}) copy-start(bf16[512,1792]{1,0:T(8,128)(2,1)} %get-tuple-element.14) | copy-start | bytes 5505028
  105.1 3.9 %copy-start.4 = (bf16[512,1024]{1,0:T(8,128)(2,1)S(1)}, bf16[512,1024]{1,0:T(8,128)(2,1)}, u32[]{:S(2)}) copy-start(bf16[512,1024]{1,0:T(8,128)(2,1)} %get-tuple-element.15) | copy-start | bytes 3145732
  109.1 3.9 %copy-start.2 = (bf16[64,1024]{1,0:T(8,128)(2,1)S(1)}, bf16[64,1024]{1,0:T(8,128)(2,1)}, u32[]{:S(2)}) copy-start(bf16[64,1024]{1,0:T(8,128)(2,1)} %get-tuple-element.20) | copy-start | bytes 393220
where the time goes:
time: 114 us
  Pallas kernels  98.2 us (86%)
  matrix products  14.2 us (12%)
    pallas_call x1, Pallas kernels, grid_device(): pl.pallas_call(functools.partial(exchange_kernel, n_row, n_col), out_shap...  98.2 us
    dot_general x3, matrix products, rows_dot(): lax.dot_general(x, y, ROWS_CONTRACT, preferred_element_type=jnp.float32)  14.2 us

commit v1 on v0

--- a/solution.py
+++ b/solution.py
@@ -142,6 +142,7 @@
     far_v,
     far_hid_v,
     mix_own_v,
+    mix_acc_v,
     mix_send_v,
     mix_recv_v,
     load_tok_sem,
@@ -150,12 +151,16 @@
     z_recv,
     yt_send,
     yt_recv,
+    zf_send,
+    zf_recv,
     core_send,
     core_recv,
     x_send,
     x_recv,
     near_send,
     near_recv,
+    nearh_send,
+    nearh_recv,
     y_send,
     y_recv,
     yh_send,
@@ -202,10 +207,12 @@
     load_cot = pltpu.make_async_copy(cot_in, cot_v.at[0], load_tok_sem.at[1])
     load_tok.start()
     load_cot.start()
-    for pair in range(2):
-        for array in range(3):
+    def start_weights(pairs):
+        for array, pair in pairs:
             for part in (2 * pair, 2 * pair + 1):
                 load_weight(array, part).start()
+
+    start_weights([(0, 0)])
 
     barrier = pltpu.get_barrier_semaphore()
     peers = [core_id, x_id, y_id] + [z_ids[b] for b in range(1, blocks)]
@@ -218,17 +225,25 @@
         return remote(buffer.at[0], buffer.at[b], z_send.at[array, b], z_recv.at[array, b], z_ids[b])
 
     load_tok.wait()
-    for b in range(1, blocks):
+    z_copy(0, 1).start()
+    load_cot.wait()
+    z_copy(1, 1).start()
+    for b in range(2, blocks):
         z_copy(0, b).start()
-    load_cot.wait()
-    for b in range(1, blocks):
         z_copy(1, b).start()
 
-    def yt_copy(b, array):
+    def yt_copy(array):
         if array == 0:
             lanes = pl.ds(pl.multiple_of(far_layer * half_feats, 128), half_feats)
-            return remote(tok_v.at[b, :, lanes], tok_far.at[b], yt_send.at[b, 0], yt_recv.at[b, 0], y_id)
-        return remote(cot_v.at[b], cot_far.at[b], yt_send.at[b, 1], yt_recv.at[b, 1], y_id)
+            return remote(tok_v.at[0, :, lanes], tok_far.at[0], yt_send.at[0], yt_recv.at[0], y_id)
+        return remote(cot_v.at[0], cot_far.at[0], yt_send.at[1], yt_recv.at[1], y_id)
+
+    yt_copy(0).start()
+    yt_copy(1).start()
+
+    def zf_copy(array, b):
+        buffer = (tok_far, cot_far)[array]
+        return remote(buffer.at[0], buffer.at[b], zf_send.at[array, b], zf_recv.at[array, b], z_ids[b])
 
     def out_rows(b, far):
         return pl.ds(pl.multiple_of((b + far * blocks) * rows, rows), rows)
@@ -244,11 +259,13 @@
     def x_copy(u, a):
         return remote(x_send_v.at[u, a], x_recv_v.at[u, a], x_send.at[u, a], x_recv.at[u, a], x_id)
 
-    def near_copy(u):
-        return remote(near_v.at[core, u], near_v.at[core, u], near_send.at[u], near_recv.at[u], core_id)
-
-    def near_arrival(u):
-        return remote(near_v.at[other, u], near_v.at[other, u], near_send.at[u], near_recv.at[u], core_id)
+    def near_copy(u, side):
+        ref = near_v.at[side, u, 0:2]
+        return remote(ref, ref, near_send.at[u], near_recv.at[u], core_id)
+
+    def nearh_copy(u, side):
+        ref = near_v.at[side, u, 2]
+        return remote(ref, ref, nearh_send.at[u], nearh_recv.at[u], core_id)
 
     def y_copy(u):
         return remote(near_v.at[core, u, 0:2], far_v.at[core, u], y_send.at[u], y_recv.at[u], y_id)
@@ -324,21 +341,38 @@
             @pl.when((b == static_b) & (q == 0))
             def _():
                 z_copy(0, static_b).wait_recv()
-                z_copy(1, static_b).wait_recv()
 
         @pl.when(q == 0)
         def _():
             own_lanes = pl.ds(pl.multiple_of(layer * half_feats, 128), half_feats)
-            yt_copy(b, 0).start()
-            yt_copy(b, 1).start()
             send_out(tok_v.at[b, :, own_lanes], tok_out.at[out_rows(b, 0), :], 0)
-            send_out(cot_v.at[b], cot_out.at[out_rows(b, 0), :], 1)
 
         wait_weight(u, 0)
+
+        @pl.when(u == 0)
+        def _():
+            start_weights([(1, 0), (2, 0)])
+
         products(u, 0)
         wait_weight(u, 1)
+
+        @pl.when(u == 0)
+        def _():
+            start_weights([(0, 1), (1, 1), (2, 1)])
+
         products(u, 1)
         finish(u, 0)
+
+        for static_b in range(1, blocks):
+
+            @pl.when((b == static_b) & (q == 0))
+            def _():
+                z_copy(1, static_b).wait_recv()
+
+        @pl.when(q == 0)
+        def _():
+            send_out(cot_v.at[b], cot_out.at[out_rows(b, 0), :], 1)
+
         wait_weight(u, 2)
         products(u, 2)
         finish(u, 1)
@@ -346,72 +380,96 @@
 
     row_step = 16
 
-    def combine(u):
+    def over_rows(body):
+        def some_rows(i, carry):
+            body(pl.ds(pl.multiple_of(i * row_step, row_step), row_step))
+            return carry
+
+        lax.fori_loop(0, rows // row_step, some_rows, 0)
+
+    def activate(u):
         q, b = u % 2, u // 2
-        for a in range(3):
-            x_copy(u, a).wait_recv()
-
-        def some_rows(i, carry):
-            span = pl.ds(pl.multiple_of(i * row_step, row_step), row_step)
+        x_copy(u, 0).wait_recv()
+        x_copy(u, 1).wait_recv()
+
+        def body(span):
             gate_sum = own_v[u, 0, span, :] + f32(x_recv_v[u, 0, span, :])
             up_sum = own_v[u, 1, span, :] + f32(x_recv_v[u, 1, span, :])
-            hidden_grad = own_v[u, 2, span, :] + f32(x_recv_v[u, 2, span, :])
             sigmoid_gate = jax.nn.sigmoid(gate_sum)
             swish = gate_sum * sigmoid_gate
             near_v[core, u, 2, span, :] = bf16(swish * up_sum)
-            near_v[core, u, 1, span, :] = bf16(hidden_grad * swish)
-            near_v[core, u, 0, span, :] = bf16(
-                hidden_grad * up_sum * sigmoid_gate * (1.0 + gate_sum * (1.0 - sigmoid_gate))
+            own_v[u, 0, span, :] = up_sum * sigmoid_gate * (1.0 + gate_sum * (1.0 - sigmoid_gate))
+            own_v[u, 1, span, :] = swish
+
+        over_rows(body)
+        nearh_copy(u, core).start()
+
+        @pl.when(q == far_layer)
+        def _():
+            yh_copy(u, b).start()
+
+        @pl.when(q == layer)
+        def _():
+            hid_to_out(near_v.at[core, u, 2], b, core, 0)
+
+    def mix_part(u):
+        q, b = u % 2, u // 2
+        nearh_copy(u, other).wait_recv()
+
+        @pl.when(q == layer)
+        def _():
+            hid_to_out(near_v.at[other, u, 2], b, other, 0)
+
+        part = jnp.zeros((rows, feats), jnp.float32)
+        for side in range(2):
+            part = part + jnp.dot(
+                near_v[side, u, 2], down_v[2 * q + side], preferred_element_type=jnp.float32
             )
-            return carry
-
-        lax.fori_loop(0, rows // row_step, some_rows, 0)
-        near_copy(u).start()
+
+        @pl.when(q == 0)
+        def _():
+            mix_acc_v[...] = part
+
+        @pl.when(u == 1)
+        def _():
+            mix_own_v[...] = mix_acc_v[...] + part
+
+        @pl.when((q == 1) & (b > 0))
+        def _():
+            mix_send_v[b] = bf16(mix_acc_v[...] + part)
+
+        for static_b in range(1, blocks):
+
+            @pl.when((q == 1) & (b == static_b))
+            def _():
+                mix_copy(static_b).start()
+
+    def factors(u):
+        x_copy(u, 2).wait_recv()
+
+        def body(span):
+            hidden_grad = own_v[u, 2, span, :] + f32(x_recv_v[u, 2, span, :])
+            near_v[core, u, 0, span, :] = bf16(hidden_grad * own_v[u, 0, span, :])
+            near_v[core, u, 1, span, :] = bf16(hidden_grad * own_v[u, 1, span, :])
+
+        over_rows(body)
+        near_copy(u, core).start()
         y_copy(u).start()
-
-        @pl.when(q == far_layer)
-        def _():
-            yh_copy(u, b).start()
-
         grads_out((near_v.at[core, u, 0], near_v.at[core, u, 1]), u, core, 0)
 
-        @pl.when(q == layer)
-        def _():
-            hid_to_out(near_v.at[core, u, 2], b, core, 0)
-
     def near_arrived(u):
-        q, b = u % 2, u // 2
-        near_arrival(u).wait_recv()
+        near_copy(u, other).wait_recv()
         grads_out((near_v.at[other, u, 0], near_v.at[other, u, 1]), u, other, 0)
 
-        @pl.when(q == layer)
-        def _():
-            hid_to_out(near_v.at[other, u, 2], b, other, 0)
-
-        @pl.when(q == 1)
-        def _():
-            total = jnp.zeros((rows, feats), jnp.float32)
-            for half in range(2):
-                for side in range(2):
-                    total = total + jnp.dot(
-                        near_v[side, 2 * b + half, 2],
-                        down_v[2 * half + side],
-                        preferred_element_type=jnp.float32,
-                    )
-
-            @pl.when(b == 0)
-            def _():
-                mix_own_v[...] = total
-
-            @pl.when(b > 0)
-            def _():
-                mix_send_v[b] = bf16(total)
-
-            for static_b in range(1, blocks):
-
-                @pl.when(b == static_b)
-                def _():
-                    mix_copy(static_b).start()
+        @pl.when(u == 1)
+        def _():
+            yt_copy(0).wait_recv()
+            yt_copy(1).wait_recv()
+            for b in range(1, blocks):
+                zf_copy(0, b).start()
+                zf_copy(1, b).start()
+            send_out(tok_far.at[0], tok_out.at[out_rows(0, 1), :], 0)
+            send_out(cot_far.at[0], cot_out.at[out_rows(0, 1), :], 1)
 
     def far_arrived(u):
         q, b = u % 2, u // 2
@@ -425,13 +483,6 @@
             fwdh_copy(b).start()
             hid_to_out(far_hid_v.at[core, b], b, core, 1)
 
-        @pl.when(q == 0)
-        def _():
-            yt_copy(b, 0).wait_recv()
-            yt_copy(b, 1).wait_recv()
-            send_out(tok_far.at[b], tok_out.at[out_rows(b, 1), :], 0)
-            send_out(cot_far.at[b], cot_out.at[out_rows(b, 1), :], 1)
-
     def forwarded(u):
         q, b = u % 2, u // 2
         fwd_arrival(u).wait_recv()
@@ -442,7 +493,15 @@
             fwdh_arrival(b).wait_recv()
             hid_to_out(far_hid_v.at[other, b], b, other, 1)
 
-    stages = ((compute_unit, 0), (combine, 2), (near_arrived, 3), (far_arrived, 4), (forwarded, 5))
+    stages = (
+        (activate, 2),
+        (compute_unit, 0),
+        (mix_part, 2),
+        (factors, 2),
+        (near_arrived, 3),
+        (far_arrived, 4),
+        (forwarded, 5),
+    )
 
     def step(s, carry):
         for stage, lag in stages:
@@ -462,13 +521,20 @@
     mixed_out[...] = bf16(total)
 
     for b in range(1, blocks):
-        z_copy(0, b).wait_send()
-        z_copy(1, b).wait_send()
+        zf_copy(0, b).wait_recv()
+        zf_copy(1, b).wait_recv()
+        send_out(tok_far.at[b], tok_out.at[out_rows(b, 1), :], 0)
+        send_out(cot_far.at[b], cot_out.at[out_rows(b, 1), :], 1)
+
+    for array in range(2):
+        yt_copy(array).wait_send()
+        for b in range(1, blocks):
+            z_copy(array, b).wait_send()
+            zf_copy(array, b).wait_send()
+    for b in range(1, blocks):
         mix_copy(b).wait_send()
 
     def drain_block(b, carry):
-        yt_copy(b, 0).wait_send()
-        yt_copy(b, 1).wait_send()
         yh_copy(2 * b, b).wait_send()
         fwdh_copy(b).wait_send()
         return carry
@@ -477,7 +543,8 @@
         for a in range(3):
             core_copy(u, a).wait_send()
             x_copy(u, a).wait_send()
-        near_copy(u).wait_send()
+        near_copy(u, core).wait_send()
+        nearh_copy(u, core).wait_send()
         y_copy(u).wait_send()
         fwd_copy(u).wait_send()
         return carry
@@ -486,6 +553,47 @@
     lax.fori_loop(0, units, drain_unit, 0)
     for slot, out in enumerate((tok_out, cot_out, hid_out, dgate_out, dup_out)):
         pltpu.make_async_copy(out, out, out_sem.at[slot]).wait()
+
+
+def gradient_kernel(tok, cot, hidden, d_gate, d_up, grad_gate, grad_up, grad_down, tok_turned):
+    @pl.when(pl.program_id(0) == 0)
+    def _():
+        tok_turned[...] = tok[...].T
+
+    turned = tok_turned[...]
+    grad_gate[...] = bf16(jnp.dot(turned, d_gate[...], preferred_element_type=jnp.float32))
+    grad_up[...] = bf16(jnp.dot(turned, d_up[...], preferred_element_type=jnp.float32))
+    grad_down[...] = bf16(rows_dot(hidden[...], cot[...]))
+
+
+def gradients(tok, cot, hidden, d_gate, d_up):
+    all_rows, half_feats = tok.shape
+    feats, half_hid, hid = cot.shape[1], hidden.shape[1], d_gate.shape[1]
+    steps = max(n for n in range(1, 8) if half_hid % (128 * n) == 0)
+    wide, thin = hid // steps, half_hid // steps
+    narrow = jnp.bfloat16
+    return pl.pallas_call(
+        gradient_kernel,
+        grid=(steps,),
+        out_shape=[
+            jax.ShapeDtypeStruct((half_feats, hid), narrow),
+            jax.ShapeDtypeStruct((half_feats, hid), narrow),
+            jax.ShapeDtypeStruct((half_hid, feats), narrow),
+        ],
+        in_specs=[
+            pl.BlockSpec((all_rows, half_feats), lambda i: (0, 0)),
+            pl.BlockSpec((all_rows, feats), lambda i: (0, 0)),
+            pl.BlockSpec((all_rows, thin), lambda i: (0, i)),
+            pl.BlockSpec((all_rows, wide), lambda i: (0, i)),
+            pl.BlockSpec((all_rows, wide), lambda i: (0, i)),
+        ],
+        out_specs=[
+            pl.BlockSpec((half_feats, wide), lambda i: (0, i)),
+            pl.BlockSpec((half_feats, wide), lambda i: (0, i)),
+            pl.BlockSpec((thin, feats), lambda i: (i, 0)),
+        ],
+        scratch_shapes=[pltpu.VMEM((half_feats, all_rows), narrow)],
+    )(tok, cot, hidden, d_gate, d_up)
 
 
 def grid_device(n_row, n_col, tokens, w_gate, w_up, w_down, cotangent):
@@ -514,18 +622,23 @@
         pltpu.VMEM((2, units, 2, rows, quarter), narrow),
         pltpu.VMEM((2, blocks, rows, quarter), narrow),
         pltpu.VMEM((rows, feats), wide),
+        pltpu.VMEM((rows, feats), wide),
         pltpu.VMEM((blocks, rows, feats), narrow),
         pltpu.VMEM((blocks, rows, feats), narrow),
         dma((2,)),
         dma((3, 4)),
         dma((2, blocks)),
         dma((2, blocks)),
-        dma((blocks, 2)),
-        dma((blocks, 2)),
+        dma((2,)),
+        dma((2,)),
+        dma((2, blocks)),
+        dma((2, blocks)),
         dma((units, 3)),
         dma((units, 3)),
         dma((units, 3)),
         dma((units, 3)),
+        dma((units,)),
+        dma((units,)),
         dma((units,)),
         dma((units,)),
         dma((units,)),
@@ -557,9 +670,7 @@
             collective_id=0, has_side_effects=True, vmem_limit_bytes=VMEM_LIMIT
         ),
     )(tokens, w_gate, w_up, w_down, cotangent)
-    grad_gate = bf16(rows_dot(tok, d_gate))
-    grad_up = bf16(rows_dot(tok, d_up))
-    grad_down = bf16(rows_dot(hidden, cot))
+    grad_gate, grad_up, grad_down = gradients(tok, cot, hidden, d_gate, d_up)
     return (mixed, grad_gate, grad_up, grad_down)
 
 

time: 114 us -> 95.2 us (0.84)
  the two profiles are of different devices: /device:TPU:9 before, /device:TPU:0 now
where the time goes in v1:
time: 95.2 us; the launch traced here: 94.9 us
  Pallas kernels  93.5 us (98%)
    pallas_call x1, Pallas kernels, grid_device(): pl.pallas_call(functools.partial(exchange_kernel, n_row, n_col), out_shap...  82.1 us
    pallas_call x1, Pallas kernels, gradients(): pl.pallas_call(gradient_kernel, grid=(steps,), out_shape=[jax.ShapeDtypeS...  11.5 us

profile of v1, /device:TPU:0, one launch (start us, length us, event | category | flops | bytes accessed | tf_op | source)
XLA Modules:
  0.0 94.9 jit_solution(9335434636733473516)
XLA Ops:
  0.6 82.1 %shard_map.84 = (bf16[64,1024]{1,0:T(8,128)(2,1)}, bf16[512,512]{1,0:T(8,128)(2,1)}, bf16[512,1024]{1,0:T(8,128)(2,1)}, bf16[512,1792]{1,0:T(8,128)(2,1)}, bf16[...) custom-call(bf16[64,1024]{1,0:T(8,128)(2,1)} %tok_in.1, bf16[1024,3584]{1,0:T(8,128)(2,1)} %gate_in.1, ...), custom_call_target="tpu_custom_call" | custom-call | tf_op jit(solution)/shard_map/pallas_call | solution.py:656
  82.7 0.0 copy-start
  82.7 11.5 %shard_map.85 = (bf16[512,3584]{1,0:T(8,128)(2,1)}, bf16[512,3584]{1,0:T(8,128)(2,1)}, bf16[1792,1024]{1,0:T(8,128)(2,1)}) custom-call(bf16[512,512]{1,0:T(8,128)(2,1)} %get-tuple-element.14.tok, bf16[512,1024]{1,0:T(8,128)(2,1)} %get-tuple-element.15.cot, bf16[512,1792]{1,0:T(8,128)(2,1)} %get-tuple-element.16.hidden, ...), custom_call_target="tpu_custom_call" | custom-call | tf_op jit(solution)/shard_map/pallas_call | solution.py:575
  94.2 0.0 copy-done
  94.2 0.7 copy.10
Async XLA Ops:
  82.7 11.5 %copy-start = (bf16[64,1024]{1,0:T(8,128)(2,1)S(1)}, bf16[64,1024]{1,0:T(8,128)(2,1)}, u32[]{:S(2)}) copy-start(bf16[64,1024]{1,0:T(8,128)(2,1)} %get-tuple-element.26) | copy-start | bytes 393220

commit v2 on v1

v2 whole, which is shorter than its diff:
```python
import functools

import jax
import jax.numpy as jnp
from jax import lax
from jax.experimental import pallas as pl
from jax.experimental.pallas import tpu as pltpu
from jax.sharding import PartitionSpec as P

COLS_CONTRACT = (((1,), (1,)), ((), ()))
ROWS_CONTRACT = (((0,), (0,)), ((), ()))


def gate_grads(hidden_grad, gate_sum, up_sum):
    sigmoid_gate = jax.nn.sigmoid(gate_sum)
    d_gate = (hidden_grad * up_sum * sigmoid_gate * (1.0 + gate_sum * (1.0 - sigmoid_gate))).astype(
        jnp.bfloat16
    )
    d_up = (hidden_grad * gate_sum * sigmoid_gate).astype(jnp.bfloat16)
    return (d_gate, d_up)


def layered_device(tokens, w_gate, w_up, w_down, cotangent):
    hid_width = w_gate.shape[1]
    token_rows = lax.all_gather(tokens, "col", axis=0, tiled=True)
    row_piece = token_rows
    joined = lax.psum_scatter(
        jnp.concatenate(
            [
                jnp.dot(row_piece, w_gate, preferred_element_type=jnp.float32),
                jnp.dot(row_piece, w_up, preferred_element_type=jnp.float32),
            ],
            axis=1,
        ).astype(jnp.bfloat16),
        "row",
        scatter_dimension=0,
        tiled=True,
    ).astype(jnp.float32)
    gate_sum = joined[:, :hid_width]
    up_sum = joined[:, hid_width:]
    hidden = (jax.nn.silu(gate_sum) * up_sum).astype(jnp.bfloat16)
    hidden_rows = lax.all_gather(hidden, "row", axis=0, tiled=True)
    row_piece = hidden_rows
    mixed = lax.psum_scatter(
        jnp.dot(row_piece, w_down, preferred_element_type=jnp.float32).astype(jnp.bfloat16),
        "col",
        scatter_dimension=0,
        tiled=True,
    )
    cot_rows = lax.all_gather(cotangent, "col", axis=0, tiled=True)
    row_piece = cot_rows
    hidden_grad = lax.psum_scatter(
        lax.dot_general(
            row_piece, w_down, COLS_CONTRACT, preferred_element_type=jnp.float32
        ).astype(jnp.bfloat16),
        "row",
        scatter_dimension=0,
        tiled=True,
    ).astype(jnp.float32)
    d_gate, d_up = gate_grads(hidden_grad, gate_sum, up_sum)
    d_gate_rows, d_up_rows = (
        lax.all_gather(d_gate, "row", axis=0, tiled=True),
        lax.all_gather(d_up, "row", axis=0, tiled=True),
    )
    down_term = lax.dot_general(
        hidden_rows, cot_rows, ROWS_CONTRACT, preferred_element_type=jnp.float32
    )
    grad_down = lax.psum_scatter(
        down_term.astype(jnp.bfloat16), "depth", scatter_dimension=0, tiled=True
    )
    layer_tokens = lax.all_to_all(token_rows, "depth", split_axis=1, concat_axis=0, tiled=True)
    block_rows = token_rows.shape[0]
    empty_grad = jnp.zeros((layer_tokens.shape[1], d_gate_rows.shape[1]), jnp.float32)
    first_row = jnp.int32(0)
    gate_total = empty_grad
    up_total = empty_grad
    gate_piece = lax.all_gather(d_gate_rows, "depth", axis=0, tiled=True)
    up_piece = lax.all_gather(d_up_rows, "depth", axis=0, tiled=True)
    for sub_index in range(gate_piece.shape[0] // block_rows):
        gate_block = gate_piece[sub_index * block_rows : (sub_index + 1) * block_rows]
        up_block = up_piece[sub_index * block_rows : (sub_index + 1) * block_rows]
        offset = first_row + sub_index * block_rows
        tok_block = lax.dynamic_slice_in_dim(layer_tokens, offset, block_rows, 0)
        gate_part = lax.optimization_barrier(
            lax.dot_general(
                tok_block, gate_block, ROWS_CONTRACT, preferred_element_type=jnp.float32
            ).astype(jnp.bfloat16)
        )
        up_part = lax.optimization_barrier(
            lax.dot_general(
                tok_block, up_block, ROWS_CONTRACT, preferred_element_type=jnp.float32
            ).astype(jnp.bfloat16)
        )
        gate_total = gate_total + gate_part.astype(jnp.float32)
        up_total = up_total + up_part.astype(jnp.float32)
    return (mixed, gate_total.astype(jnp.bfloat16), up_total.astype(jnp.bfloat16), grad_down)


MESH = pl.DeviceIdType.MESH
VMEM_LIMIT = 52_000_000
VMEM_GRADS = 32_000_000


def f32(x):
    return x.astype(jnp.float32)


def bf16(x):
    return x.astype(jnp.bfloat16)


def rows_dot(x, y):
    return lax.dot_general(x, y, ROWS_CONTRACT, preferred_element_type=jnp.float32)


def exchange_kernel(
    n_row,
    n_col,
    tok_in,
    gate_in,
    up_in,
    down_in,
    cot_in,
    mix_v,
    tok_v,
    tok_far,
    cot_v,
    grad_v,
    hid_v,
    gate_v,
    up_v,
    down_v,
    core_send_v,
    core_recv_v,
    own_v,
    x_send_v,
    x_recv_v,
    mix_acc_v,
    mix_send_v,
    mix_recv_v,
    load_tok_sem,
    load_w_sem,
    z_send,
    z_recv,
    yt_send,
    yt_recv,
    zf_send,
    zf_recv,
    core_send,
    core_recv,
    x_send,
    x_recv,
    near_send,
    near_recv,
    nearh_send,
    nearh_recv,
    y_send,
    y_recv,
    yh_send,
    yh_recv,
    fwd_send,
    fwd_recv,
    fwdh_send,
    fwdh_recv,
    mix_send,
    mix_recv,
):
    row, col, layer = lax.axis_index("row"), lax.axis_index("col"), lax.axis_index("depth")
    core = row % 2
    other = 1 - core
    far_layer = 1 - layer
    blocks, rows, feats = tok_v.shape
    half_feats = tok_far.shape[2]
    quarter = gate_v.shape[2]
    units = x_send_v.shape[0]

    core_id = (row + 1 - 2 * core, col, layer)
    x_id = ((row + 2) % n_row, col, layer)
    y_id = (row, col, far_layer)
    z_ids = {
        1: (row, col + 1 - 2 * (col % 2), layer),
        2: (row, (col + 2) % n_col, layer),
        3: (row, n_col - 1 - col, layer),
    }

    def place(u):
        late, last = (u + units - 3) // units, (u + 1) // units
        second = (u + late) % 2 + last
        return second, (second + far_layer) % 2, (u + late) // 2 - (blocks - 1) * last

    def remote(src, dst, send, recv, device):
        return pltpu.make_async_remote_copy(
            src_ref=src, dst_ref=dst, send_sem=send, recv_sem=recv, device_id=device, device_id_type=MESH
        )

    def load_weight(array, part):
        source = (gate_in, up_in, down_in)[array]
        target = (gate_v, up_v, down_v)[array]
        span = pl.ds(pl.multiple_of(part * quarter, 128), quarter)
        view = source.at[span, :] if array == 2 else source.at[:, span]
        return pltpu.make_async_copy(view, target.at[part], load_w_sem.at[array, part])

    load_tok = pltpu.make_async_copy(tok_in, tok_v.at[0], load_tok_sem.at[0])
    load_cot = pltpu.make_async_copy(cot_in, cot_v.at[0, 0], load_tok_sem.at[1])
    load_tok.start()
    load_cot.start()
    def start_weights(pairs):
        for array, pair in pairs:
            for part in (2 * pair + other, 2 * pair + core):
                load_weight(array, part).start()

    first_q = far_layer
    start_weights([(0, first_q)])

    barrier = pltpu.get_barrier_semaphore()
    peers = [core_id, x_id, y_id] + [z_ids[b] for b in range(1, blocks)]
    for peer in peers:
        pl.semaphore_signal(barrier, inc=1, device_id=peer, device_id_type=MESH)

    def core_copy(u, a):
        return remote(
            core_send_v.at[u, a], core_recv_v.at[u, a], core_send.at[u, a], core_recv.at[u, a], core_id
        )

    def product(u, array, side):
        second, q, b = place(u)
        part = 2 * q + side
        if array == 2:
            return lax.dot_general(
                cot_v[0, b], down_v[part], COLS_CONTRACT, preferred_element_type=jnp.float32
            )
        weight = (gate_v, up_v)[array]
        return jnp.dot(tok_v[b], weight[part], preferred_element_type=jnp.float32)

    load_tok.wait()
    load_weight(0, 2 * first_q + other).wait()
    start_weights([(1, first_q)])
    core_send_v[0, 0] = bf16(product(0, 0, other))
    pl.semaphore_wait(barrier, len(peers))
    core_copy(0, 0).start()

    def z_copy(array, b):
        buffer = (tok_v, cot_v.at[0])[array]
        return remote(buffer.at[0], buffer.at[b], z_send.at[array, b], z_recv.at[array, b], z_ids[b])

    z_copy(0, 1).start()
    load_cot.wait()
    z_copy(1, 1).start()
    for b in range(2, blocks):
        z_copy(0, b).start()
        z_copy(1, b).start()

    def yt_copy(array):
        if array == 0:
            lanes = pl.ds(pl.multiple_of(far_layer * half_feats, 128), half_feats)
            return remote(tok_v.at[0, :, lanes], tok_far.at[0], yt_send.at[0], yt_recv.at[0], y_id)
        return remote(cot_v.at[0, 0], cot_v.at[1, 0], yt_send.at[1], yt_recv.at[1], y_id)

    yt_copy(0).start()
    yt_copy(1).start()

    def zf_copy(array, b):
        buffer = (tok_far, cot_v.at[1])[array]
        return remote(buffer.at[0], buffer.at[b], zf_send.at[array, b], zf_recv.at[array, b], z_ids[b])

    def part_rows(half):
        return pl.ds(half * (rows // 2), rows // 2)

    def x_copy(u, a, half):
        span = part_rows(half)
        return remote(
            x_send_v.at[u, a, span],
            x_recv_v.at[u, a, span],
            x_send.at[u, a, half],
            x_recv.at[u, a, half],
            x_id,
        )

    def near_copy(u, half, side):
        second, q, b = place(u)
        ref = grad_v.at[side, q, :, 0, b, part_rows(half)]
        return remote(ref, ref, near_send.at[u, half], near_recv.at[u, half], core_id)

    def hid_slot(second):
        return 2 - 2 * second

    def nearh_copy(u, half, side):
        second, q, b = place(u)
        ref = hid_v.at[side, hid_slot(second), b, part_rows(half)]
        return remote(ref, ref, nearh_send.at[u, half], nearh_recv.at[u, half], core_id)

    def y_copy(u, half):
        second, q, b = place(u)
        span = part_rows(half)
        return remote(
            grad_v.at[core, q, :, 0, b, span],
            grad_v.at[core, q, :, 1, b, span],
            y_send.at[u, half],
            y_recv.at[u, half],
            y_id,
        )

    def y_arrival(u, half):
        second, q, b = place(u)
        ref = grad_v.at[core, 1 - q, :, 1, b, part_rows(half)]
        return remote(ref, ref, y_send.at[u, half], y_recv.at[u, half], y_id)

    def yh_copy(b, half):
        span = part_rows(half)
        return remote(
            hid_v.at[core, 2, b, span],
            hid_v.at[core, 1, b, span],
            yh_send.at[b, half],
            yh_recv.at[b, half],
            y_id,
        )

    def fwd_copy(u, half, side):
        second, q, b = place(u)
        ref = grad_v.at[side, 1 - q, :, 1, b, part_rows(half)]
        return remote(ref, ref, fwd_send.at[u, half], fwd_recv.at[u, half], core_id)

    def fwdh_copy(b, half, side):
        ref = hid_v.at[side, 1, b, part_rows(half)]
        return remote(ref, ref, fwdh_send.at[b, half], fwdh_recv.at[b, half], core_id)

    def mix_copy(b):
        return remote(mix_send_v.at[b], mix_recv_v.at[b], mix_send.at[b], mix_recv.at[b], z_ids[b])

    def products(u, array):
        def for_other():
            core_send_v[u, array] = bf16(product(u, array, other))
            core_copy(u, array).start()

        if array == 0:
            pl.when(u > 0)(for_other)
        else:
            for_other()
        own_v[u, array] = product(u, array, core)

    def finish(u, array):
        core_copy(u, array).wait_recv()
        total = own_v[u, array] + f32(core_recv_v[u, array])
        own_v[u, array] = total
        x_send_v[u, array] = bf16(total)

        @pl.when(u < units - 1)
        def _():
            for half in range(2):
                x_copy(u, array, half).start()

    def wait_weight(u, array):
        second, q, b = place(u)
        if array == 0:

            @pl.when(u == 1)
            def _():
                load_weight(array, 2 * q + other).wait()
        else:

            @pl.when(b == 0)
            def _():
                load_weight(array, 2 * q + other).wait()

        @pl.when(b == 0)
        def _():
            load_weight(array, 2 * q + core).wait()

    def compute_unit(u):
        second, q, b = place(u)

        for static_b in range(1, blocks):

            @pl.when((b == static_b) & (second == 0))
            def _():
                z_copy(0, static_b).wait_recv()

        wait_weight(u, 0)

        @pl.when(u == 0)
        def _():
            start_weights([(2, first_q)])

        products(u, 0)

        @pl.when(u == 0)
        def _():
            finish(u, 0)

        wait_weight(u, 1)

        @pl.when(u == 0)
        def _():
            start_weights([(0, layer), (1, layer), (2, layer)])

        products(u, 1)

        @pl.when(u > 0)
        def _():
            finish(u, 0)

        for static_b in range(1, blocks):

            @pl.when((b == static_b) & (second == 0))
            def _():
                z_copy(1, static_b).wait_recv()

        wait_weight(u, 2)
        products(u, 2)
        finish(u, 1)
        finish(u, 2)

        @pl.when(u == units - 1)
        def _():
            for half in range(2):
                for array in range(3):
                    x_copy(u, array, half).start()

    row_step = 16

    def over_rows(half, body):
        base = half * (rows // 2)

        def some_rows(i, carry):
            body(pl.ds(pl.multiple_of(base + i * row_step, row_step), row_step))
            return carry

        lax.fori_loop(0, rows // 2 // row_step, some_rows, 0)

    def activate(u, half):
        second, q, b = place(u)
        x_copy(u, 0, half).wait_recv()
        x_copy(u, 1, half).wait_recv()

        def body(span):
            gate_sum = own_v[u, 0, span, :] + f32(x_recv_v[u, 0, span, :])
            up_sum = own_v[u, 1, span, :] + f32(x_recv_v[u, 1, span, :])
            sigmoid_gate = jax.nn.sigmoid(gate_sum)
            swish = gate_sum * sigmoid_gate
            hid_v[core, hid_slot(second), b, span, :] = bf16(swish * up_sum)
            own_v[u, 0, span, :] = up_sum * sigmoid_gate * (1.0 + gate_sum * (1.0 - sigmoid_gate))
            own_v[u, 1, span, :] = swish

        over_rows(half, body)
        nearh_copy(u, half, core).start()

        @pl.when(second == 0)
        def _():
            yh_copy(b, half).start()

    def factors(u, half):
        second, q, b = place(u)
        x_copy(u, 2, half).wait_recv()

        def body(span):
            hidden_grad = own_v[u, 2, span, :] + f32(x_recv_v[u, 2, span, :])
            grad_v[core, q, 0, 0, b, span, :] = bf16(hidden_grad * own_v[u, 0, span, :])
            grad_v[core, q, 1, 0, b, span, :] = bf16(hidden_grad * own_v[u, 1, span, :])

        over_rows(half, body)
        y_copy(u, half).start()
        near_copy(u, half, core).start()

    def elementwise(u):
        for half in range(2):
            activate(u, half)
            factors(u, half)

    def mix_part(u):
        second, q, b = place(u)
        for half in range(2):
            nearh_copy(u, half, other).wait_recv()

        part = jnp.zeros((rows, feats), jnp.float32)
        for side in range(2):
            part = part + jnp.dot(
                hid_v[side, hid_slot(second), b], down_v[2 * q + side], preferred_element_type=jnp.float32
            )

        @pl.when(second == 0)
        def _():
            mix_acc_v[b] = part

        @pl.when((second == 1) & (b == 0))
        def _():
            mix_acc_v[0] = mix_acc_v[0] + part

        @pl.when((second == 1) & (b > 0))
        def _():
            mix_send_v[b] = bf16(mix_acc_v[b] + part)

        for static_b in range(1, blocks):

            @pl.when((second == 1) & (b == static_b))
            def _():
                mix_copy(static_b).start()

    def near_arrived(u):
        for half in range(2):
            near_copy(u, half, other).wait_recv()

        @pl.when(u == 1)
        def _():
            yt_copy(0).wait_recv()
            yt_copy(1).wait_recv()
            for b in range(1, blocks):
                zf_copy(0, b).start()
                zf_copy(1, b).start()

    def far_arrived(u):
        second, q, b = place(u)
        for half in range(2):

            @pl.when(second == 0)
            def _():
                yh_copy(b, half).wait_recv()
                fwdh_copy(b, half, core).start()

            y_arrival(u, half).wait_recv()
            fwd_copy(u, half, core).start()

    def forwarded(u):
        second, q, b = place(u)
        for half in range(2):

            @pl.when(second == 0)
            def _():
                fwdh_copy(b, half, other).wait_recv()

            fwd_copy(u, half, other).wait_recv()

    stages = (
        (elementwise, 2),
        (compute_unit, 0),
        (mix_part, 2),
        (near_arrived, 3),
        (far_arrived, 4),
        (forwarded, 5),
    )

    def step(s, carry):
        for stage, lag in stages:

            @pl.when((s >= lag) & (s < units + lag))
            def _():
                stage(s - lag)

        return carry

    lax.fori_loop(0, units + stages[-1][1], step, 0)

    total = mix_acc_v[0]
    for b in [*range(2, blocks), 1]:
        mix_copy(b).wait_recv()
        total = total + f32(mix_recv_v[b])
    mix_v[...] = bf16(total)

    for b in range(1, blocks):
        zf_copy(0, b).wait_recv()
        zf_copy(1, b).wait_recv()

    for array in range(2):
        yt_copy(array).wait_send()
        for b in range(1, blocks):
            z_copy(array, b).wait_send()
            zf_copy(array, b).wait_send()
    for b in range(1, blocks):
        mix_copy(b).wait_send()

    def drain_block(b, carry):
        for half in range(2):
            yh_copy(b, half).wait_send()
            fwdh_copy(b, half, core).wait_send()
        return carry

    def drain_unit(u, carry):
        for a in range(3):
            core_copy(u, a).wait_send()
        for half in range(2):
            for a in range(3):
                x_copy(u, a, half).wait_send()
            near_copy(u, half, core).wait_send()
            nearh_copy(u, half, core).wait_send()
            y_copy(u, half).wait_send()
            fwd_copy(u, half, core).wait_send()
        return carry

    lax.fori_loop(0, blocks, drain_block, 0)
    lax.fori_loop(0, units, drain_unit, 0)


def gradient_kernel(
    mix_v,
    tok_v,
    tok_far,
    cot_v,
    grad_v,
    hid_v,
    mixed,
    grad_gate,
    grad_up,
    grad_down,
    tok_turned,
    hid_turned,
    wide_v,
    down_v,
    mix_sem,
    wide_sem,
    down_sem,
):
    layer = lax.axis_index("depth")
    blocks, rows, half_feats = tok_far.shape
    half_rows = blocks * rows
    quarter = grad_v.shape[-1]
    mix_copy = pltpu.make_async_copy(mix_v, mixed, mix_sem)
    mix_copy.start()
    own = tok_v[:, :, pl.ds(pl.multiple_of(layer * half_feats, 128), half_feats)]
    tok_turned[:, :half_rows] = own.reshape(half_rows, half_feats).T
    tok_turned[:, half_rows:] = tok_far[...].reshape(half_rows, half_feats).T

    def wide_copy(part, array):
        target = (grad_gate, grad_up)[array]
        lanes = pl.ds(part * quarter, quarter)
        return pltpu.make_async_copy(
            wide_v.at[array, part % 2], target.at[:, lanes], wide_sem.at[array, part % 2]
        )

    def down_copy(part):
        side, half = part // 2, part % 2
        return pltpu.make_async_copy(
            down_v.at[half],
            grad_down.at[pl.ds(side * quarter, quarter), pl.ds(half * half_feats, half_feats)],
            down_sem.at[half],
        )

    for part in range(4):
        q, side = part // 2, part % 2
        for array in range(2):
            if part >= 2:
                wide_copy(part - 2, array).wait()
            factor = grad_v[side, q, array].reshape(2 * half_rows, quarter)
            wide_v[array, part % 2] = bf16(
                jnp.dot(tok_turned[...], factor, preferred_element_type=jnp.float32)
            )
            wide_copy(part, array).start()
        side, half = part // 2, part % 2
        if part >= 2:
            down_copy(part - 2).wait()
        if half == 0:
            hid_turned[...] = hid_v[side, 0:2].reshape(2 * half_rows, quarter).T
        cot = cot_v[:, :, :, half * half_feats : (half + 1) * half_feats]
        down_v[half] = bf16(
            jnp.dot(
                hid_turned[...],
                cot.reshape(2 * half_rows, half_feats),
                preferred_element_type=jnp.float32,
            )
        )
        down_copy(part).start()
    for part in (2, 3):
        wide_copy(part, 0).wait()
        wide_copy(part, 1).wait()
        down_copy(part).wait()
    mix_copy.wait()


def gradients(mixed, tok, tok_far, cot, grad, hid):
    blocks, rows, half_feats = tok_far.shape
    all_rows = 2 * blocks * rows
    feats, quarter = tok.shape[2], grad.shape[-1]
    narrow = jnp.bfloat16
    dma = pltpu.SemaphoreType.DMA
    return pl.pallas_call(
        gradient_kernel,
        out_shape=[
            jax.ShapeDtypeStruct(mixed.shape, narrow),
            jax.ShapeDtypeStruct((half_feats, 4 * quarter), narrow),
            jax.ShapeDtypeStruct((half_feats, 4 * quarter), narrow),
            jax.ShapeDtypeStruct((2 * quarter, feats), narrow),
        ],
        in_specs=[pl.BlockSpec(memory_space=pltpu.VMEM)] * 6,
        out_specs=[pl.BlockSpec(memory_space=pl.ANY)] * 4,
        scratch_shapes=[
            pltpu.VMEM((half_feats, all_rows), narrow),
            pltpu.VMEM((quarter, all_rows), narrow),
            pltpu.VMEM((2, 2, half_feats, quarter), narrow),
            pltpu.VMEM((2, quarter, half_feats), narrow),
            dma,
            dma((2, 2)),
            dma((2,)),
        ],
        compiler_params=pltpu.CompilerParams(vmem_limit_bytes=VMEM_GRADS),
    )(mixed, tok, tok_far, cot, grad, hid)


def grid_device(n_row, n_col, tokens, w_gate, w_up, w_down, cotangent):
    rows, feats = tokens.shape
    hid = w_gate.shape[1]
    quarter = hid // 4
    blocks = n_col
    units = 2 * blocks
    all_rows = 2 * blocks * rows
    narrow, wide = jnp.bfloat16, jnp.float32
    dma = pltpu.SemaphoreType.DMA
    scratch = [
        pltpu.VMEM((4, feats, quarter), narrow),
        pltpu.VMEM((4, feats, quarter), narrow),
        pltpu.VMEM((4, quarter, feats), narrow),
        pltpu.VMEM((units, 3, rows, quarter), narrow),
        pltpu.VMEM((units, 3, rows, quarter), narrow),
        pltpu.VMEM((units, 3, rows, quarter), wide),
        pltpu.VMEM((units, 3, rows, quarter), narrow),
        pltpu.VMEM((units, 3, rows, quarter), narrow),
        pltpu.VMEM((blocks, rows, feats), wide),
        pltpu.VMEM((blocks, rows, feats), narrow),
        pltpu.VMEM((blocks, rows, feats), narrow),
        dma((2,)),
        dma((3, 4)),
        dma((2, blocks)),
        dma((2, blocks)),
        dma((2,)),
        dma((2,)),
        dma((2, blocks)),
        dma((2, blocks)),
        dma((units, 3)),
        dma((units, 3)),
        dma((units, 3, 2)),
        dma((units, 3, 2)),
    ]
    scratch += [dma((units, 2))] * 6
    scratch += [dma((blocks, 2))] * 2
    scratch += [dma((units, 2))] * 2
    scratch += [
        dma((blocks, 2)),
        dma((blocks, 2)),
        dma((blocks,)),
        dma((blocks,)),
    ]
    results = pl.pallas_call(
        functools.partial(exchange_kernel, n_row, n_col),
        out_shape=[
            pltpu.VMEM((rows, feats), narrow),
            pltpu.VMEM((blocks, rows, feats), narrow),
            pltpu.VMEM((blocks, rows, feats // 2), narrow),
            pltpu.VMEM((2, blocks, rows, feats), narrow),
            pltpu.VMEM((2, 2, 2, 2, blocks, rows, quarter), narrow),
            pltpu.VMEM((2, 3, blocks, rows, quarter), narrow),
        ],
        in_specs=[pl.BlockSpec(memory_space=pl.ANY)] * 5,
        out_specs=[pl.BlockSpec(memory_space=pltpu.VMEM)] * 6,
        scratch_shapes=scratch,
        compiler_params=pltpu.CompilerParams(
            collective_id=0, has_side_effects=True, vmem_limit_bytes=VMEM_LIMIT
        ),
    )(tokens, w_gate, w_up, w_down, cotangent)
    return tuple(gradients(*results))


def solution(mesh):
    placed = (
        P(("col", "depth"), "row"),
        P("row", "col"),
        P("row", "col"),
        P("col", "row"),
        P(("col", "depth"), "row"),
    )
    n_row, n_col = mesh.shape["row"], mesh.shape["col"]
    if (n_row, n_col, mesh.shape["depth"]) == (4, 4, 2):
        per_device = functools.partial(grid_device, n_row, n_col)
    else:
        per_device = layered_device
    return jax.shard_map(
        per_device,
        mesh=mesh,
        in_specs=placed,
        out_specs=(
            P(("col", "depth"), "row"),
            P(("row", "depth"), "col"),
            P(("row", "depth"), "col"),
            P(("col", "depth"), "row"),
        ),
        check_vma=False,
    )
```

time: 95.2 us -> 86.5 us (0.909)
  Pallas kernels: 93.5 us -> 85.7 us
    pallas_call x1, Pallas kernels: 82.1 us -> 77.2 us  [grid_device(): pl.pallas_call(functools.partial(exchange_kernel, n_row, n_col), out_shap...]
    pallas_call x1, Pallas kernels: 11.5 us -> 8.5 us  [gradients(): pl.pallas_call(gradient_kernel, out_shape=[jax.ShapeDtypeStruct(mixed.sha...]
where the time goes in v2:
time: 86.5 us; the launch traced here: 86.3 us
  Pallas kernels  85.7 us (99%)
    pallas_call x1, Pallas kernels, grid_device(): pl.pallas_call(functools.partial(exchange_kernel, n_row, n_col), out_shap...  77.2 us
    pallas_call x1, Pallas kernels, gradients(): pl.pallas_call(gradient_kernel, out_shape=[jax.ShapeDtypeStruct(mixed.sha...  8.5 us

profile of v2, /device:TPU:0, one launch (start us, length us, event | category | flops | bytes accessed | tf_op | source)
XLA Modules:
  0.0 86.3 jit_solution(12490916414923876510)
XLA Ops:
  0.6 77.2 %shard_map.84 = (bf16[64,1024]{1,0:T(8,128)(2,1)S(1)}, bf16[4,64,1024]{2,1,0:T(8,128)(2,1)S(1)}, bf16[4,64,512]{2,1,0:T(8,128)(2,1)S(1)}, bf16[2,4,64,1024]{3,2,...) custom-call(bf16[64,1024]{1,0:T(8,128)(2,1)} %tok_in.1, ...), custom_call_target="tpu_custom_call" | custom-call | tf_op jit(solution)/shard_map/pallas_call | solution.py:739
  77.8 8.5 %shard_map.85 = (bf16[64,1024]{1,0:T(8,128)(2,1)}, bf16[512,3584]{1,0:T(8,128)(2,1)}, bf16[512,3584]{1,0:T(8,128)(2,1)}, bf16[1792,1024]{1,0:T(8,128)(2,1)}) custom-call(bf16[64,1024]{1,0:T(8,128)(2,1)S(1)} %get-tuple-element.10.mix_v, bf16[4,64,1024]{2,1,0:T(8,128)(2,1)S(1)} %get-tuple-element.11.tok_v, bf16[4,64,512]{2,1,0:T(8,128)(2,1)S(1)} %get-tuple-element.12.tok_far, ...), custom_call_target="tpu_custom_call" | custom-call | tf_op jit(solution)/shard_map/pallas_call | solution.py:673

commit v3 on v2

v3 whole, which is shorter than its diff:
```python
import functools

import jax
import jax.numpy as jnp
from jax import lax
from jax.experimental import pallas as pl
from jax.experimental.pallas import tpu as pltpu
from jax.sharding import PartitionSpec as P

COLS_CONTRACT = (((1,), (1,)), ((), ()))
ROWS_CONTRACT = (((0,), (0,)), ((), ()))


def gate_grads(hidden_grad, gate_sum, up_sum):
    sigmoid_gate = jax.nn.sigmoid(gate_sum)
    d_gate = (hidden_grad * up_sum * sigmoid_gate * (1.0 + gate_sum * (1.0 - sigmoid_gate))).astype(
        jnp.bfloat16
    )
    d_up = (hidden_grad * gate_sum * sigmoid_gate).astype(jnp.bfloat16)
    return (d_gate, d_up)


def layered_device(tokens, w_gate, w_up, w_down, cotangent):
    hid_width = w_gate.shape[1]
    token_rows = lax.all_gather(tokens, "col", axis=0, tiled=True)
    row_piece = token_rows
    joined = lax.psum_scatter(
        jnp.concatenate(
            [
                jnp.dot(row_piece, w_gate, preferred_element_type=jnp.float32),
                jnp.dot(row_piece, w_up, preferred_element_type=jnp.float32),
            ],
            axis=1,
        ).astype(jnp.bfloat16),
        "row",
        scatter_dimension=0,
        tiled=True,
    ).astype(jnp.float32)
    gate_sum = joined[:, :hid_width]
    up_sum = joined[:, hid_width:]
    hidden = (jax.nn.silu(gate_sum) * up_sum).astype(jnp.bfloat16)
    hidden_rows = lax.all_gather(hidden, "row", axis=0, tiled=True)
    row_piece = hidden_rows
    mixed = lax.psum_scatter(
        jnp.dot(row_piece, w_down, preferred_element_type=jnp.float32).astype(jnp.bfloat16),
        "col",
        scatter_dimension=0,
        tiled=True,
    )
    cot_rows = lax.all_gather(cotangent, "col", axis=0, tiled=True)
    row_piece = cot_rows
    hidden_grad = lax.psum_scatter(
        lax.dot_general(
            row_piece, w_down, COLS_CONTRACT, preferred_element_type=jnp.float32
        ).astype(jnp.bfloat16),
        "row",
        scatter_dimension=0,
        tiled=True,
    ).astype(jnp.float32)
    d_gate, d_up = gate_grads(hidden_grad, gate_sum, up_sum)
    d_gate_rows, d_up_rows = (
        lax.all_gather(d_gate, "row", axis=0, tiled=True),
        lax.all_gather(d_up, "row", axis=0, tiled=True),
    )
    down_term = lax.dot_general(
        hidden_rows, cot_rows, ROWS_CONTRACT, preferred_element_type=jnp.float32
    )
    grad_down = lax.psum_scatter(
        down_term.astype(jnp.bfloat16), "depth", scatter_dimension=0, tiled=True
    )
    layer_tokens = lax.all_to_all(token_rows, "depth", split_axis=1, concat_axis=0, tiled=True)
    block_rows = token_rows.shape[0]
    empty_grad = jnp.zeros((layer_tokens.shape[1], d_gate_rows.shape[1]), jnp.float32)
    first_row = jnp.int32(0)
    gate_total = empty_grad
    up_total = empty_grad
    gate_piece = lax.all_gather(d_gate_rows, "depth", axis=0, tiled=True)
    up_piece = lax.all_gather(d_up_rows, "depth", axis=0, tiled=True)
    for sub_index in range(gate_piece.shape[0] // block_rows):
        gate_block = gate_piece[sub_index * block_rows : (sub_index + 1) * block_rows]
        up_block = up_piece[sub_index * block_rows : (sub_index + 1) * block_rows]
        offset = first_row + sub_index * block_rows
        tok_block = lax.dynamic_slice_in_dim(layer_tokens, offset, block_rows, 0)
        gate_part = lax.optimization_barrier(
            lax.dot_general(
                tok_block, gate_block, ROWS_CONTRACT, preferred_element_type=jnp.float32
            ).astype(jnp.bfloat16)
        )
        up_part = lax.optimization_barrier(
            lax.dot_general(
                tok_block, up_block, ROWS_CONTRACT, preferred_element_type=jnp.float32
            ).astype(jnp.bfloat16)
        )
        gate_total = gate_total + gate_part.astype(jnp.float32)
        up_total = up_total + up_part.astype(jnp.float32)
    return (mixed, gate_total.astype(jnp.bfloat16), up_total.astype(jnp.bfloat16), grad_down)


MESH = pl.DeviceIdType.MESH
VMEM_LIMIT = 50_000_000
VMEM_GRADS = 32_000_000


def f32(x):
    return x.astype(jnp.float32)


def bf16(x):
    return x.astype(jnp.bfloat16)


def rows_dot(x, y):
    return lax.dot_general(x, y, ROWS_CONTRACT, preferred_element_type=jnp.float32)


def exchange_kernel(
    n_row,
    n_col,
    tok_in,
    gate_in,
    up_in,
    down_in,
    cot_in,
    mix_v,
    tok_turned,
    down_grad_v,
    grad_v,
    tok_v,
    tok_far,
    cot_v,
    hid_v,
    hid_turned,
    gate_v,
    up_v,
    down_v,
    core_send_v,
    core_recv_v,
    own_v,
    x_send_v,
    x_recv_v,
    mix_acc_v,
    mix_send_v,
    mix_recv_v,
    load_tok_sem,
    load_w_sem,
    sent,
    late,
    z_recv,
    yt_recv,
    core_recv,
    x_recv,
    nearh_recv,
    y_recv,
    yh_recv,
    mix_recv,
):
    row, col, layer = lax.axis_index("row"), lax.axis_index("col"), lax.axis_index("depth")
    core = row % 2
    other = 1 - core
    far_layer = 1 - layer
    blocks, rows, feats = tok_v.shape
    half_feats = tok_far.shape[2]
    quarter = gate_v.shape[2]
    units = x_send_v.shape[0]

    core_id = (row + 1 - 2 * core, col, layer)
    x_id = ((row + 2) % n_row, col, layer)
    y_id = (row, col, far_layer)
    z_ids = {
        1: (row, col + 1 - 2 * (col % 2), layer),
        2: (row, (col + 2) % n_col, layer),
        3: (row, n_col - 1 - col, layer),
    }

    def place(u):
        skip, final = (u + units - 3) // units, (u + 1) // units
        second = (u + skip) % 2 + final
        return second, (second + far_layer) % 2, (u + skip) // 2 - (blocks - 1) * final

    def remote(src, dst, send, recv, device):
        return pltpu.make_async_remote_copy(
            src_ref=src, dst_ref=dst, send_sem=send, recv_sem=recv, device_id=device, device_id_type=MESH
        )

    def weight_sem(array, second, own):
        if second == 0 and array == 0:
            return load_w_sem.at[own]
        return load_w_sem.at[1 + array + 3 * second]

    def load_weight(array, second):
        for own, side in ((0, other), (1, core)):
            part = 2 * ((second + far_layer) % 2) + side
            source = (gate_in, up_in, down_in)[array]
            target = (gate_v, up_v, down_v)[array]
            span = pl.ds(pl.multiple_of(part * quarter, 128), quarter)
            view = source.at[span, :] if array == 2 else source.at[:, span]
            pltpu.make_async_copy(view, target.at[part], weight_sem(array, second, own)).start()

    def weight_wait(array, second, own):
        source = (gate_in, up_in, down_in)[array]
        target = (gate_v, up_v, down_v)[array]
        single = second == 0 and array == 0
        wide = quarter if single else 2 * quarter
        view = source.at[0:wide, :] if array == 2 else source.at[:, 0:wide]
        pltpu.make_async_copy(view, view, weight_sem(array, second, own)).wait()

    load_tok = pltpu.make_async_copy(tok_in, tok_v.at[0], load_tok_sem.at[0])
    load_cot = pltpu.make_async_copy(cot_in, cot_v.at[0, 0], load_tok_sem.at[1])
    load_tok.start()
    load_cot.start()
    load_weight(0, 0)

    barrier = pltpu.get_barrier_semaphore()
    peers = [core_id, x_id, y_id] + [z_ids[b] for b in range(1, blocks)]
    for peer in peers:
        pl.semaphore_signal(barrier, inc=1, device_id=peer, device_id_type=MESH)

    def core_copy(u, a):
        return remote(
            core_send_v.at[u, a], core_recv_v.at[u, a], sent.at[0], core_recv.at[u, a], core_id
        )

    def product(u, array, side):
        second, q, b = place(u)
        part = 2 * q + side
        if array == 2:
            return lax.dot_general(
                cot_v[0, b], down_v[part], COLS_CONTRACT, preferred_element_type=jnp.float32
            )
        weight = (gate_v, up_v)[array]
        return jnp.dot(tok_v[b], weight[part], preferred_element_type=jnp.float32)

    load_tok.wait()
    weight_wait(0, 0, 0)
    load_weight(1, 0)
    core_send_v[0, 0] = bf16(product(0, 0, other))
    pl.semaphore_wait(barrier, len(peers))
    core_copy(0, 0).start()

    def z_copy(array, b):
        buffer = (tok_v, cot_v.at[0])[array]
        return remote(buffer.at[0], buffer.at[b], sent.at[1 + array], z_recv.at[array, b], z_ids[b])

    z_copy(0, 1).start()
    load_cot.wait()
    z_copy(1, 1).start()
    for b in range(2, blocks):
        z_copy(0, b).start()
        z_copy(1, b).start()

    def yt_copy(array):
        if array == 0:
            lanes = pl.ds(pl.multiple_of(far_layer * half_feats, 128), half_feats)
            return remote(tok_v.at[0, :, lanes], tok_far.at[0], sent.at[3], yt_recv.at[0], y_id)
        return remote(cot_v.at[0, 0], cot_v.at[1, 0], sent.at[4], yt_recv.at[1], y_id)

    yt_copy(0).start()
    yt_copy(1).start()

    def zf_copy(array, b):
        buffer = (tok_far, cot_v.at[1])[array]
        return remote(buffer.at[0], buffer.at[b], sent.at[5 + array], late.at[array], z_ids[b])

    def part_rows(half):
        return pl.ds(half * (rows // 2), rows // 2)

    def x_copy(u, a, half):
        span = part_rows(half)
        return remote(
            x_send_v.at[u, a, span],
            x_recv_v.at[u, a, span],
            sent.at[7],
            x_recv.at[u, a // 2, half],
            x_id,
        )

    def x_pair_arrival(u, half):
        ref = x_recv_v.at[u, 0:2, part_rows(half)]
        return remote(ref, ref, sent.at[7], x_recv.at[u, 0, half], x_id)

    def near_copy(u, half):
        second, q, b = place(u)
        ref = grad_v.at[core, q, :, 0, b, part_rows(half)]
        return remote(ref, ref, sent.at[8], late.at[2], core_id)

    def hid_slot(second):
        return 2 - 2 * second

    def nearh_copy(u, half):
        second, q, b = place(u)
        ref = hid_v.at[core, hid_slot(second), b, part_rows(half)]
        return remote(ref, ref, sent.at[9], nearh_recv.at[u], core_id)

    def nearh_arrival(u):
        second, q, b = place(u)
        ref = hid_v.at[other, hid_slot(second), b]
        return remote(ref, ref, sent.at[9], nearh_recv.at[u], core_id)

    def y_slot(u, half):
        return u + half * ((u + 1) // units)

    def y_copy(u, half):
        second, q, b = place(u)
        span = part_rows(half)
        return remote(
            grad_v.at[core, q, :, 0, b, span],
            grad_v.at[core, q, :, 1, b, span],
            sent.at[10],
            y_recv.at[y_slot(u, half)],
            y_id,
        )

    def y_arrival(u, span, slot):
        second, q, b = place(u)
        ref = grad_v.at[core, 1 - q, :, 1, b, span]
        return remote(ref, ref, sent.at[10], y_recv.at[slot], y_id)

    def yh_copy(b, half):
        span = part_rows(half)
        return remote(
            hid_v.at[core, 2, b, span], hid_v.at[core, 1, b, span], sent.at[11], yh_recv.at[b], y_id
        )

    def yh_arrival(b):
        ref = hid_v.at[core, 1, b]
        return remote(ref, ref, sent.at[11], yh_recv.at[b], y_id)

    def fwd_copy(u, span):
        second, q, b = place(u)
        ref = grad_v.at[core, 1 - q, :, 1, b, span]
        return remote(ref, ref, sent.at[12], late.at[3], core_id)

    def fwdh_copy(b):
        ref = hid_v.at[core, 1, b]
        return remote(ref, ref, sent.at[13], late.at[4], core_id)

    def mix_copy(b):
        return remote(mix_send_v.at[b], mix_recv_v.at[b], sent.at[14], mix_recv.at[b], z_ids[b])

    def all_sent(ref, slot):
        remote(ref, ref, sent.at[slot], late.at[0], core_id).wait_send()

    def all_arrived(ref, slot):
        remote(ref, ref, sent.at[0], late.at[slot], core_id).wait_recv()

    def products(u, array):
        def for_other():
            core_send_v[u, array] = bf16(product(u, array, other))
            core_copy(u, array).start()

        if array == 0:
            pl.when(u > 0)(for_other)
        else:
            for_other()
        own_v[u, array] = product(u, array, core)

    def finish(u, array):
        core_copy(u, array).wait_recv()
        total = own_v[u, array] + f32(core_recv_v[u, array])
        own_v[u, array] = total
        x_send_v[u, array] = bf16(total)

        @pl.when(u < units - 1)
        def _():
            for half in range(2):
                x_copy(u, array, half).start()

    def wait_weight(u, array):
        for second in range(2):

            @pl.when(u == second)
            def _():
                weight_wait(array, second, 1)

    def compute_unit(u):
        second, q, b = place(u)

        for static_b in range(1, blocks):

            @pl.when((b == static_b) & (second == 0))
            def _():
                z_copy(0, static_b).wait_recv()

        wait_weight(u, 0)

        @pl.when(u == 0)
        def _():
            load_weight(2, 0)

        products(u, 0)

        @pl.when(u == 0)
        def _():
            finish(u, 0)

        wait_weight(u, 1)

        @pl.when(u == 0)
        def _():
            for array in range(3):
                load_weight(array, 1)

        products(u, 1)

        @pl.when(u > 0)
        def _():
            finish(u, 0)

        for static_b in range(1, blocks):

            @pl.when((b == static_b) & (second == 0))
            def _():
                z_copy(1, static_b).wait_recv()

        wait_weight(u, 2)
        products(u, 2)
        finish(u, 1)
        finish(u, 2)

        @pl.when(u == units - 1)
        def _():
            for half in range(2):
                for array in range(3):
                    x_copy(u, array, half).start()

    row_step = 16

    def over_rows(half, body):
        base = half * (rows // 2)

        def some_rows(i, carry):
            body(pl.ds(pl.multiple_of(base + i * row_step, row_step), row_step))
            return carry

        lax.fori_loop(0, rows // 2 // row_step, some_rows, 0)

    def activate(u, half):
        second, q, b = place(u)
        x_pair_arrival(u, half).wait_recv()

        def body(span):
            gate_sum = own_v[u, 0, span, :] + f32(x_recv_v[u, 0, span, :])
            up_sum = own_v[u, 1, span, :] + f32(x_recv_v[u, 1, span, :])
            sigmoid_gate = jax.nn.sigmoid(gate_sum)
            swish = gate_sum * sigmoid_gate
            hid_v[core, hid_slot(second), b, span, :] = bf16(swish * up_sum)
            own_v[u, 0, span, :] = up_sum * sigmoid_gate * (1.0 + gate_sum * (1.0 - sigmoid_gate))
            own_v[u, 1, span, :] = swish

        over_rows(half, body)
        nearh_copy(u, half).start()

        @pl.when(second == 0)
        def _():
            yh_copy(b, half).start()

    def factors(u, half):
        second, q, b = place(u)
        x_copy(u, 2, half).wait_recv()

        def body(span):
            hidden_grad = own_v[u, 2, span, :] + f32(x_recv_v[u, 2, span, :])
            grad_v[core, q, 0, 0, b, span, :] = bf16(hidden_grad * own_v[u, 0, span, :])
            grad_v[core, q, 1, 0, b, span, :] = bf16(hidden_grad * own_v[u, 1, span, :])

        over_rows(half, body)
        y_copy(u, half).start()
        near_copy(u, half).start()

    def elementwise(u):
        for half in range(2):
            activate(u, half)
            factors(u, half)

    def mix_part(u):
        second, q, b = place(u)
        nearh_arrival(u).wait_recv()

        part = jnp.zeros((rows, feats), jnp.float32)
        for side in range(2):
            part = part + jnp.dot(
                hid_v[side, hid_slot(second), b], down_v[2 * q + side], preferred_element_type=jnp.float32
            )

        @pl.when(second == 0)
        def _():
            mix_acc_v[b] = part

        @pl.when((second == 1) & (b == 0))
        def _():
            mix_acc_v[0] = mix_acc_v[0] + part

        @pl.when((second == 1) & (b > 0))
        def _():
            mix_send_v[b] = bf16(mix_acc_v[b] + part)

        for static_b in range(1, blocks):

            @pl.when((second == 1) & (b == static_b))
            def _():
                mix_copy(static_b).start()

    def spread_far():
        yt_copy(0).wait_recv()
        yt_copy(1).wait_recv()
        for b in range(1, blocks):
            zf_copy(0, b).start()
            zf_copy(1, b).start()

    def far_arrived(u):
        second, q, b = place(u)

        @pl.when(second == 0)
        def _():
            yh_arrival(b).wait_recv()
            fwdh_copy(b).start()

        whole = pl.ds(0, rows)
        y_arrival(u, whole, u).wait_recv()
        fwd_copy(u, whole).start()

    def last_far(half):
        span = part_rows(half)
        y_arrival(units - 1, span, units - 1 + half).wait_recv()
        fwd_copy(units - 1, span).start()

    def turn_tokens():
        all_arrived(tok_far.at[1:blocks], 0)
        all_arrived(cot_v.at[1, 1:blocks], 1)
        half_rows = blocks * rows
        own = tok_v[:, :, pl.ds(pl.multiple_of(layer * half_feats, 128), half_feats)]
        tok_turned[:, :half_rows] = own.reshape(half_rows, half_feats).T
        tok_turned[:, half_rows:] = tok_far[...].reshape(half_rows, half_feats).T

    def down_grad(side, half):
        if half == 0:
            hid_turned[...] = hid_v[side, 0:2].reshape(2 * blocks * rows, quarter).T
        lanes = slice(half * half_feats, (half + 1) * half_feats)
        down_grad_v[side * quarter : (side + 1) * quarter, lanes] = bf16(
            jnp.dot(
                hid_turned[...],
                cot_v[:, :, :, lanes].reshape(2 * blocks * rows, half_feats),
                preferred_element_type=jnp.float32,
            )
        )

    stages = ((elementwise, 2), (compute_unit, 0), (mix_part, 2), (far_arrived, 4))

    def step(s, carry):
        for stage, lag in stages:

            @pl.when((s >= lag) & (s < units + lag))
            def _():
                stage(s - lag)

        pl.when(s == 4)(spread_far)
        pl.when(s == units)(turn_tokens)
        return carry

    lax.fori_loop(0, units + 2, step, 0)
    far_arrived(units - 2)
    all_arrived(hid_v.at[other, 1], 4)
    down_grad(0, 0)
    last_far(0)
    down_grad(0, 1)
    down_grad(1, 0)
    last_far(1)
    down_grad(1, 1)

    total = mix_acc_v[0]
    for b in [*range(2, blocks), 1]:
        mix_copy(b).wait_recv()
        total = total + f32(mix_recv_v[b])
    mix_v[...] = bf16(total)

    all_arrived(grad_v.at[other, :, :, 0], 2)
    all_arrived(grad_v.at[other, :, :, 1], 3)
    all_sent(core_send_v, 0)
    all_sent(tok_v.at[1:blocks], 1)
    all_sent(cot_v.at[0, 1:blocks], 2)
    all_sent(tok_far.at[0], 3)
    all_sent(cot_v.at[0, 0], 4)
    all_sent(tok_far.at[1:blocks], 5)
    all_sent(cot_v.at[1, 1:blocks], 6)
    all_sent(x_send_v, 7)
    all_sent(grad_v.at[core, :, :, 0], 8)
    all_sent(hid_v.at[core, 0:2], 9)
    all_sent(grad_v.at[core, :, :, 0], 10)
    all_sent(hid_v.at[core, 2], 11)
    all_sent(grad_v.at[core, :, :, 1], 12)
    all_sent(hid_v.at[core, 1], 13)
    all_sent(mix_send_v.at[1:blocks], 14)


def gradient_kernel(
    mix_v, tok_turned, down_grad_v, grad_v, mixed, grad_gate, grad_up, grad_down, wide_v, done, wide_sem
):
    quarter = grad_v.shape[-1]
    all_rows = tok_turned.shape[1]
    mix_copy = pltpu.make_async_copy(mix_v, mixed, done.at[0])
    down_copy = pltpu.make_async_copy(down_grad_v, grad_down, done.at[1])
    mix_copy.start()
    down_copy.start()
    copies = []
    for part in range(4):
        q, side = part // 2, part % 2
        for array in range(2):
            slot = len(copies) % 4
            if len(copies) >= 4:
                copies[-4].wait()
            factor = grad_v[side, q, array].reshape(all_rows, quarter)
            wide_v[slot] = bf16(jnp.dot(tok_turned[...], factor, preferred_element_type=jnp.float32))
            target = (grad_gate, grad_up)[array]
            copies.append(
                pltpu.make_async_copy(
                    wide_v.at[slot], target.at[:, pl.ds(part * quarter, quarter)], wide_sem.at[slot]
                )
            )
            copies[-1].start()
    for copy in copies[-4:]:
        copy.wait()
    mix_copy.wait()
    down_copy.wait()


def gradients(mixed, tok, down_grad, grad):
    half_feats, quarter = tok.shape[0], grad.shape[-1]
    narrow = jnp.bfloat16
    dma = pltpu.SemaphoreType.DMA
    return pl.pallas_call(
        gradient_kernel,
        out_shape=[
            jax.ShapeDtypeStruct(mixed.shape, narrow),
            jax.ShapeDtypeStruct((half_feats, 4 * quarter), narrow),
            jax.ShapeDtypeStruct((half_feats, 4 * quarter), narrow),
            jax.ShapeDtypeStruct(down_grad.shape, narrow),
        ],
        in_specs=[pl.BlockSpec(memory_space=pltpu.VMEM)] * 4,
        out_specs=[pl.BlockSpec(memory_space=pl.ANY)] * 4,
        scratch_shapes=[pltpu.VMEM((4, half_feats, quarter), narrow), dma((2,)), dma((4,))],
        compiler_params=pltpu.CompilerParams(vmem_limit_bytes=VMEM_GRADS),
    )(mixed, tok, down_grad, grad)


def grid_device(n_row, n_col, tokens, w_gate, w_up, w_down, cotangent):
    rows, feats = tokens.shape
    hid = w_gate.shape[1]
    quarter = hid // 4
    blocks = n_col
    units = 2 * blocks
    all_rows = 2 * blocks * rows
    narrow, wide = jnp.bfloat16, jnp.float32
    dma = pltpu.SemaphoreType.DMA
    results = pl.pallas_call(
        functools.partial(exchange_kernel, n_row, n_col),
        out_shape=[
            pltpu.VMEM((rows, feats), narrow),
            pltpu.VMEM((feats // 2, all_rows), narrow),
            pltpu.VMEM((hid // 2, feats), narrow),
            pltpu.VMEM((2, 2, 2, 2, blocks, rows, quarter), narrow),
        ],
        in_specs=[pl.BlockSpec(memory_space=pl.ANY)] * 5,
        out_specs=[pl.BlockSpec(memory_space=pltpu.VMEM)] * 4,
        scratch_shapes=[
            pltpu.VMEM((blocks, rows, feats), narrow),
            pltpu.VMEM((blocks, rows, feats // 2), narrow),
            pltpu.VMEM((2, blocks, rows, feats), narrow),
            pltpu.VMEM((2, 3, blocks, rows, quarter), narrow),
            pltpu.VMEM((quarter, all_rows), narrow),
            pltpu.VMEM((4, feats, quarter), narrow),
            pltpu.VMEM((4, feats, quarter), narrow),
            pltpu.VMEM((4, quarter, feats), narrow),
            pltpu.VMEM((units, 3, rows, quarter), narrow),
            pltpu.VMEM((units, 3, rows, quarter), narrow),
            pltpu.VMEM((units, 3, rows, quarter), wide),
            pltpu.VMEM((units, 3, rows, quarter), narrow),
            pltpu.VMEM((units, 3, rows, quarter), narrow),
            pltpu.VMEM((blocks, rows, feats), wide),
            pltpu.VMEM((blocks, rows, feats), narrow),
            pltpu.VMEM((blocks, rows, feats), narrow),
            dma((2,)),
            dma((7,)),
            dma((15,)),
            dma((5,)),
            dma((2, blocks)),
            dma((2,)),
            dma((units, 3)),
            dma((units, 2, 2)),
            dma((units,)),
            dma((units + 1,)),
            dma((blocks,)),
            dma((blocks,)),
        ],
        compiler_params=pltpu.CompilerParams(
            collective_id=0, has_side_effects=True, vmem_limit_bytes=VMEM_LIMIT
        ),
    )(tokens, w_gate, w_up, w_down, cotangent)
    return tuple(gradients(*results))


def solution(mesh):
    placed = (
        P(("col", "depth"), "row"),
        P("row", "col"),
        P("row", "col"),
        P("col", "row"),
        P(("col", "depth"), "row"),
    )
    n_row, n_col = mesh.shape["row"], mesh.shape["col"]
    if (n_row, n_col, mesh.shape["depth"]) == (4, 4, 2):
        per_device = functools.partial(grid_device, n_row, n_col)
    else:
        per_device = layered_device
    return jax.shard_map(
        per_device,
        mesh=mesh,
        in_specs=placed,
        out_specs=(
            P(("col", "depth"), "row"),
            P(("row", "depth"), "col"),
            P(("row", "depth"), "col"),
            P(("col", "depth"), "row"),
        ),
        check_vma=False,
    )
```

time: 86.5 us -> 81.7 us (0.945)
  Pallas kernels: 85.7 us -> 80.9 us
    pallas_call x1, Pallas kernels: 77.2 us -> 74.7 us  [grid_device(): pl.pallas_call(functools.partial(exchange_kernel, n_row, n_col), out_shap...]
    pallas_call x1, Pallas kernels: 8.5 us -> 6.18 us  [gradients(): pl.pallas_call(gradient_kernel, out_shape=[jax.ShapeDtypeStruct(mixed.sha...]
where the time goes in v3:
time: 81.7 us; the launch traced here: 81.5 us
  Pallas kernels  80.9 us (99%)
    pallas_call x1, Pallas kernels, grid_device(): pl.pallas_call(functools.partial(exchange_kernel, n_row, n_col), out_shap...  74.7 us
    pallas_call x1, Pallas kernels, gradients(): pl.pallas_call(gradient_kernel, out_shape=[jax.ShapeDtypeStruct(mixed.sha...  6.18 us

profile of v3, /device:TPU:0, one launch (start us, length us, event | category | flops | bytes accessed | tf_op | source)
XLA Modules:
  0.0 81.5 jit_solution(2760766088278070316)
XLA Ops:
  0.6 74.7 %shard_map.84 = (bf16[64,1024]{1,0:T(8,128)(2,1)S(1)}, bf16[512,512]{1,0:T(8,128)(2,1)S(1)}, bf16[1792,1024]{1,0:T(8,128)(2,1)S(1)}, bf16[2,2,2,2,4,64,896]{6,5,4,3,2,1,0:T(8,128)(2,1)S(1)}) custom-call(bf16[64,1024]{1,0:T(8,128)(2,1)} %tok_in.1, bf16[1024,3584]{1,0:T(8,128)(2,1)} %gate_in.1, bf16[1024,3584]{1,0:T(8,128)(2,1)} %up_in.1, ...), custom_call_target="tpu_custom_call" | custom-call | tf_op jit(solution)/shard_map/pallas_call | solution.py:654
  75.3 6.2 %shard_map.85 = (bf16[64,1024]{1,0:T(8,128)(2,1)}, bf16[512,3584]{1,0:T(8,128)(2,1)}, bf16[512,3584]{1,0:T(8,128)(2,1)}, bf16[1792,1024]{1,0:T(8,128)(2,1)}) custom-call(bf16[64,1024]{1,0:T(8,128)(2,1)S(1)} %get-tuple-element.8.mix_v, bf16[512,512]{1,0:T(8,128)(2,1)S(1)} %get-tuple-element.9.tok_turned, ...), custom_call_target="tpu_custom_call" | custom-call | tf_op jit(solution)/shard_map/pallas_call | solution.py:630

commit v4 on v3

--- a/solution.py
+++ b/solution.py
@@ -149,6 +149,7 @@
     yt_recv,
     core_recv,
     x_recv,
+    x_last,
     nearh_recv,
     y_recv,
     yh_recv,
@@ -163,6 +164,9 @@
     quarter = gate_v.shape[2]
     units = x_send_v.shape[0]
 
+    core_lanes = pl.ds(pl.multiple_of(core * quarter, 128), quarter)
+    other_lanes = pl.ds(pl.multiple_of(other * quarter, 128), quarter)
+
     core_id = (row + 1 - 2 * core, col, layer)
     x_id = ((row + 2) % n_row, col, layer)
     y_id = (row, col, far_layer)
@@ -261,62 +265,54 @@
         buffer = (tok_far, cot_v.at[1])[array]
         return remote(buffer.at[0], buffer.at[b], sent.at[5 + array], late.at[array], z_ids[b])
 
-    def part_rows(half):
-        return pl.ds(half * (rows // 2), rows // 2)
-
-    def x_copy(u, a, half):
-        span = part_rows(half)
-        return remote(
-            x_send_v.at[u, a, span],
-            x_recv_v.at[u, a, span],
-            sent.at[7],
-            x_recv.at[u, a // 2, half],
-            x_id,
-        )
-
-    def x_pair_arrival(u, half):
-        ref = x_recv_v.at[u, 0:2, part_rows(half)]
-        return remote(ref, ref, sent.at[7], x_recv.at[u, 0, half], x_id)
-
-    def near_copy(u, half):
-        second, q, b = place(u)
-        ref = grad_v.at[core, q, :, 0, b, part_rows(half)]
+    last = units - 1
+    halves, pieces = 2, 4
+
+    def part_rows(part, parts):
+        return pl.ds(part * (rows // parts), rows // parts)
+
+    def x_copy(u, a, span, recv):
+        return remote(x_send_v.at[u, a, span], x_recv_v.at[u, a, span], sent.at[7], recv, x_id)
+
+    def x_sem(u, a, part):
+        return x_recv.at[u, a // 2, part]
+
+    def x_last_sem(a, part):
+        return x_last.at[a // 2, part]
+
+    def x_pair_arrival(u, span, recv):
+        ref = x_recv_v.at[u, 0:2, span]
+        return remote(ref, ref, sent.at[7], recv, x_id)
+
+    def near_copy(u, span):
+        second, q, b = place(u)
+        ref = grad_v.at[q, :, 0, b, span, core_lanes]
         return remote(ref, ref, sent.at[8], late.at[2], core_id)
 
     def hid_slot(second):
         return 2 - 2 * second
 
-    def nearh_copy(u, half):
-        second, q, b = place(u)
-        ref = hid_v.at[core, hid_slot(second), b, part_rows(half)]
-        return remote(ref, ref, sent.at[9], nearh_recv.at[u], core_id)
-
-    def nearh_arrival(u):
-        second, q, b = place(u)
-        ref = hid_v.at[other, hid_slot(second), b]
-        return remote(ref, ref, sent.at[9], nearh_recv.at[u], core_id)
-
-    def y_slot(u, half):
-        return u + half * ((u + 1) // units)
-
-    def y_copy(u, half):
-        second, q, b = place(u)
-        span = part_rows(half)
+    def nearh_copy(u, span, slot, side):
+        second, q, b = place(u)
+        ref = hid_v.at[side, hid_slot(second), b, span]
+        return remote(ref, ref, sent.at[9], nearh_recv.at[slot], core_id)
+
+    def y_copy(u, span, slot):
+        second, q, b = place(u)
         return remote(
-            grad_v.at[core, q, :, 0, b, span],
-            grad_v.at[core, q, :, 1, b, span],
+            grad_v.at[q, :, 0, b, span, core_lanes],
+            grad_v.at[q, :, 1, b, span, core_lanes],
             sent.at[10],
-            y_recv.at[y_slot(u, half)],
+            y_recv.at[slot],
             y_id,
         )
 
     def y_arrival(u, span, slot):
         second, q, b = place(u)
-        ref = grad_v.at[core, 1 - q, :, 1, b, span]
+        ref = grad_v.at[1 - q, :, 1, b, span, core_lanes]
         return remote(ref, ref, sent.at[10], y_recv.at[slot], y_id)
 
-    def yh_copy(b, half):
-        span = part_rows(half)
+    def yh_copy(b, span):
         return remote(
             hid_v.at[core, 2, b, span], hid_v.at[core, 1, b, span], sent.at[11], yh_recv.at[b], y_id
         )
@@ -327,7 +323,7 @@
 
     def fwd_copy(u, span):
         second, q, b = place(u)
-        ref = grad_v.at[core, 1 - q, :, 1, b, span]
+        ref = grad_v.at[1 - q, :, 1, b, span, core_lanes]
         return remote(ref, ref, sent.at[12], late.at[3], core_id)
 
     def fwdh_copy(b):
@@ -336,6 +332,12 @@
 
     def mix_copy(b):
         return remote(mix_send_v.at[b], mix_recv_v.at[b], sent.at[14], mix_recv.at[b], z_ids[b])
+
+    def mix_last_copy(half):
+        span = part_rows(half, halves)
+        return remote(
+            mix_send_v.at[1, span], mix_recv_v.at[1, span], sent.at[14], mix_recv.at[half], z_ids[1]
+        )
 
     def all_sent(ref, slot):
         remote(ref, ref, sent.at[slot], late.at[0], core_id).wait_send()
@@ -360,10 +362,10 @@
         own_v[u, array] = total
         x_send_v[u, array] = bf16(total)
 
-        @pl.when(u < units - 1)
-        def _():
-            for half in range(2):
-                x_copy(u, array, half).start()
+        @pl.when(u < last)
+        def _():
+            for half in range(halves):
+                x_copy(u, array, part_rows(half, halves), x_sem(u, array, half)).start()
 
     def wait_weight(u, array):
         for second in range(2):
@@ -417,64 +419,69 @@
         finish(u, 1)
         finish(u, 2)
 
-        @pl.when(u == units - 1)
-        def _():
-            for half in range(2):
+        @pl.when(u == last)
+        def _():
+            for part in range(pieces):
                 for array in range(3):
-                    x_copy(u, array, half).start()
+                    x_copy(last, array, part_rows(part, pieces), x_last_sem(array, part)).start()
 
     row_step = 16
 
-    def over_rows(half, body):
-        base = half * (rows // 2)
+    def over_rows(part, parts, body):
+        count = rows // parts
+        if count == row_step:
+            body(pl.ds(part * count, count))
+            return
 
         def some_rows(i, carry):
-            body(pl.ds(pl.multiple_of(base + i * row_step, row_step), row_step))
+            body(pl.ds(pl.multiple_of(part * count + i * row_step, row_step), row_step))
             return carry
 
-        lax.fori_loop(0, rows // 2 // row_step, some_rows, 0)
-
-    def activate(u, half):
-        second, q, b = place(u)
-        x_pair_arrival(u, half).wait_recv()
-
-        def body(span):
-            gate_sum = own_v[u, 0, span, :] + f32(x_recv_v[u, 0, span, :])
-            up_sum = own_v[u, 1, span, :] + f32(x_recv_v[u, 1, span, :])
+        lax.fori_loop(0, count // row_step, some_rows, 0)
+
+    def activate(u, part, parts, recv, slot):
+        second, q, b = place(u)
+        span = part_rows(part, parts)
+        x_pair_arrival(u, span, recv).wait_recv()
+
+        def body(lines):
+            gate_sum = own_v[u, 0, lines, :] + f32(x_recv_v[u, 0, lines, :])
+            up_sum = own_v[u, 1, lines, :] + f32(x_recv_v[u, 1, lines, :])
             sigmoid_gate = jax.nn.sigmoid(gate_sum)
             swish = gate_sum * sigmoid_gate
-            hid_v[core, hid_slot(second), b, span, :] = bf16(swish * up_sum)
-            own_v[u, 0, span, :] = up_sum * sigmoid_gate * (1.0 + gate_sum * (1.0 - sigmoid_gate))
-            own_v[u, 1, span, :] = swish
-
-        over_rows(half, body)
-        nearh_copy(u, half).start()
+            hid_v[core, hid_slot(second), b, lines, :] = bf16(swish * up_sum)
+            own_v[u, 0, lines, :] = up_sum * sigmoid_gate * (1.0 + gate_sum * (1.0 - sigmoid_gate))
+            own_v[u, 1, lines, :] = swish
+
+        over_rows(part, parts, body)
+        nearh_copy(u, span, slot, core).start()
 
         @pl.when(second == 0)
         def _():
-            yh_copy(b, half).start()
-
-    def factors(u, half):
-        second, q, b = place(u)
-        x_copy(u, 2, half).wait_recv()
-
-        def body(span):
-            hidden_grad = own_v[u, 2, span, :] + f32(x_recv_v[u, 2, span, :])
-            grad_v[core, q, 0, 0, b, span, :] = bf16(hidden_grad * own_v[u, 0, span, :])
-            grad_v[core, q, 1, 0, b, span, :] = bf16(hidden_grad * own_v[u, 1, span, :])
-
-        over_rows(half, body)
-        y_copy(u, half).start()
-        near_copy(u, half).start()
+            yh_copy(b, span).start()
+
+    def factors(u, part, parts, recv, slot):
+        second, q, b = place(u)
+        span = part_rows(part, parts)
+        x_copy(u, 2, span, recv).wait_recv()
+
+        def body(lines):
+            hidden_grad = own_v[u, 2, lines, :] + f32(x_recv_v[u, 2, lines, :])
+            grad_v[q, 0, 0, b, lines, core_lanes] = bf16(hidden_grad * own_v[u, 0, lines, :])
+            grad_v[q, 1, 0, b, lines, core_lanes] = bf16(hidden_grad * own_v[u, 1, lines, :])
+
+        over_rows(part, parts, body)
+        y_copy(u, span, slot).start()
+        near_copy(u, span).start()
 
     def elementwise(u):
-        for half in range(2):
-            activate(u, half)
-            factors(u, half)
+        for half in range(halves):
+            activate(u, half, halves, x_sem(u, 0, half), u)
+            factors(u, half, halves, x_sem(u, 2, half), u)
 
     def mix_part(u):
         second, q, b = place(u)
-        nearh_arrival(u).wait_recv()
+        nearh_copy(u, pl.ds(0, rows), u, other).wait_recv()
 
         part = jnp.zeros((rows, feats), jnp.float32)
         for side in range(2):
@@ -494,11 +501,24 @@
         def _():
             mix_send_v[b] = bf16(mix_acc_v[b] + part)
 
-        for static_b in range(1, blocks):
+        for static_b in range(2, blocks):
 
             @pl.when((second == 1) & (b == static_b))
             def _():
                 mix_copy(static_b).start()
+
+    def mix_last(half):
+        second, q, b = place(last)
+        span = part_rows(half, halves)
+        part = mix_acc_v[b, span, :]
+        for side in (core, other):
+            if side is other:
+                nearh_copy(last, span, last + half, other).wait_recv()
+            part = part + jnp.dot(
+                hid_v[side, 0, b, span, :], down_v[2 * q + side], preferred_element_type=jnp.float32
+            )
+        mix_send_v[b, span, :] = bf16(part)
+        mix_last_copy(half).start()
 
     def spread_far():
         yt_copy(0).wait_recv()
@@ -519,10 +539,10 @@
         y_arrival(u, whole, u).wait_recv()
         fwd_copy(u, whole).start()
 
-    def last_far(half):
-        span = part_rows(half)
-        y_arrival(units - 1, span, units - 1 + half).wait_recv()
-        fwd_copy(units - 1, span).start()
+    def last_far(part):
+        span = part_rows(part, pieces)
+        y_arrival(last, span, last + part).wait_recv()
+        fwd_copy(last, span).start()
 
     def turn_tokens():
         all_arrived(tok_far.at[1:blocks], 0)
@@ -536,7 +556,7 @@
         if half == 0:
             hid_turned[...] = hid_v[side, 0:2].reshape(2 * blocks * rows, quarter).T
         lanes = slice(half * half_feats, (half + 1) * half_feats)
-        down_grad_v[side * quarter : (side + 1) * quarter, lanes] = bf16(
+        down_grad_v[side, :, lanes] = bf16(
             jnp.dot(
                 hid_turned[...],
                 cot_v[:, :, :, lanes].reshape(2 * blocks * rows, half_feats),
@@ -544,12 +564,17 @@
             )
         )
 
-    stages = ((elementwise, 2), (compute_unit, 0), (mix_part, 2), (far_arrived, 4))
+    stages = (
+        (elementwise, 2, last),
+        (compute_unit, 0, units),
+        (mix_part, 2, last),
+        (far_arrived, 3, last - 1),
+    )
 
     def step(s, carry):
-        for stage, lag in stages:
-
-            @pl.when((s >= lag) & (s < units + lag))
+        for stage, lag, count in stages:
+
+            @pl.when((s >= lag) & (s < count + lag))
             def _():
                 stage(s - lag)
 
@@ -557,24 +582,36 @@
         pl.when(s == units)(turn_tokens)
         return carry
 
-    lax.fori_loop(0, units + 2, step, 0)
-    far_arrived(units - 2)
+    lax.fori_loop(0, units + 1, step, 0)
+    for part in range(pieces):
+        half = part // 2
+        activate(last, part, pieces, x_last_sem(0, part), last + half)
+        factors(last, part, pieces, x_last_sem(2, part), last + part)
+        if part == 1:
+            mix_last(0)
+    far_arrived(last - 1)
+    down_grad(core, 0)
+    last_far(0)
+    mix_last(1)
+    last_far(1)
+    down_grad(core, 1)
+    last_far(2)
     all_arrived(hid_v.at[other, 1], 4)
-    down_grad(0, 0)
-    last_far(0)
-    down_grad(0, 1)
-    down_grad(1, 0)
-    last_far(1)
-    down_grad(1, 1)
+    down_grad(other, 0)
+    last_far(3)
+    down_grad(other, 1)
 
     total = mix_acc_v[0]
-    for b in [*range(2, blocks), 1]:
+    for b in range(2, blocks):
         mix_copy(b).wait_recv()
         total = total + f32(mix_recv_v[b])
+    for half in range(halves):
+        mix_last_copy(half).wait_recv()
+    total = total + f32(mix_recv_v[1])
     mix_v[...] = bf16(total)
 
-    all_arrived(grad_v.at[other, :, :, 0], 2)
-    all_arrived(grad_v.at[other, :, :, 1], 3)
+    all_arrived(grad_v.at[:, :, 0, :, :, other_lanes], 2)
+    all_arrived(grad_v.at[:, :, 1, :, :, other_lanes], 3)
     all_sent(core_send_v, 0)
     all_sent(tok_v.at[1:blocks], 1)
     all_sent(cot_v.at[0, 1:blocks], 2)
@@ -583,11 +620,11 @@
     all_sent(tok_far.at[1:blocks], 5)
     all_sent(cot_v.at[1, 1:blocks], 6)
     all_sent(x_send_v, 7)
-    all_sent(grad_v.at[core, :, :, 0], 8)
+    all_sent(grad_v.at[:, :, 0, :, :, core_lanes], 8)
     all_sent(hid_v.at[core, 0:2], 9)
-    all_sent(grad_v.at[core, :, :, 0], 10)
+    all_sent(grad_v.at[:, :, 0, :, :, core_lanes], 10)
     all_sent(hid_v.at[core, 2], 11)
-    all_sent(grad_v.at[core, :, :, 1], 12)
+    all_sent(grad_v.at[:, :, 1, :, :, core_lanes], 12)
     all_sent(hid_v.at[core, 1], 13)
     all_sent(mix_send_v.at[1:blocks], 14)
 
@@ -595,49 +632,59 @@
 def gradient_kernel(
     mix_v, tok_turned, down_grad_v, grad_v, mixed, grad_gate, grad_up, grad_down, wide_v, done, wide_sem
 ):
-    quarter = grad_v.shape[-1]
+    half_hid = grad_v.shape[-1]
+    quarter = half_hid // 2
     all_rows = tok_turned.shape[1]
+    cut = min(half_hid, -(-half_hid // 512) * 256)
     mix_copy = pltpu.make_async_copy(mix_v, mixed, done.at[0])
-    down_copy = pltpu.make_async_copy(down_grad_v, grad_down, done.at[1])
+    down_copies = [
+        pltpu.make_async_copy(
+            down_grad_v.at[side], grad_down.at[pl.ds(side * quarter, quarter)], done.at[1 + side]
+        )
+        for side in range(2)
+    ]
     mix_copy.start()
-    down_copy.start()
+    for copy in down_copies:
+        copy.start()
     copies = []
-    for part in range(4):
-        q, side = part // 2, part % 2
+    for q in range(2):
         for array in range(2):
-            slot = len(copies) % 4
-            if len(copies) >= 4:
-                copies[-4].wait()
-            factor = grad_v[side, q, array].reshape(all_rows, quarter)
-            wide_v[slot] = bf16(jnp.dot(tok_turned[...], factor, preferred_element_type=jnp.float32))
-            target = (grad_gate, grad_up)[array]
-            copies.append(
-                pltpu.make_async_copy(
-                    wide_v.at[slot], target.at[:, pl.ds(part * quarter, quarter)], wide_sem.at[slot]
+            for start, stop in ((0, cut), (cut, half_hid)):
+                slot = len(copies) % 4
+                if len(copies) >= 4:
+                    copies[-4].wait()
+                factor = grad_v[q, array, :, :, :, start:stop].reshape(all_rows, stop - start)
+                piece = wide_v.at[slot, :, 0 : stop - start]
+                piece[...] = bf16(
+                    jnp.dot(tok_turned[...], factor, preferred_element_type=jnp.float32)
                 )
-            )
-            copies[-1].start()
+                target = (grad_gate, grad_up)[array]
+                lanes = slice(q * half_hid + start, q * half_hid + stop)
+                copies.append(pltpu.make_async_copy(piece, target.at[:, lanes], wide_sem.at[slot]))
+                copies[-1].start()
     for copy in copies[-4:]:
         copy.wait()
     mix_copy.wait()
-    down_copy.wait()
+    for copy in down_copies:
+        copy.wait()
 
 
 def gradients(mixed, tok, down_grad, grad):
-    half_feats, quarter = tok.shape[0], grad.shape[-1]
+    half_feats, half_hid = tok.shape[0], grad.shape[-1]
+    cut = min(half_hid, -(-half_hid // 512) * 256)
     narrow = jnp.bfloat16
     dma = pltpu.SemaphoreType.DMA
     return pl.pallas_call(
         gradient_kernel,
         out_shape=[
             jax.ShapeDtypeStruct(mixed.shape, narrow),
-            jax.ShapeDtypeStruct((half_feats, 4 * quarter), narrow),
-            jax.ShapeDtypeStruct((half_feats, 4 * quarter), narrow),
-            jax.ShapeDtypeStruct(down_grad.shape, narrow),
+            jax.ShapeDtypeStruct((half_feats, 2 * half_hid), narrow),
+            jax.ShapeDtypeStruct((half_feats, 2 * half_hid), narrow),
+            jax.ShapeDtypeStruct((half_hid, down_grad.shape[2]), narrow),
         ],
         in_specs=[pl.BlockSpec(memory_space=pltpu.VMEM)] * 4,
         out_specs=[pl.BlockSpec(memory_space=pl.ANY)] * 4,
-        scratch_shapes=[pltpu.VMEM((4, half_feats, quarter), narrow), dma((2,)), dma((4,))],
+        scratch_shapes=[pltpu.VMEM((4, half_feats, cut), narrow), dma((3,)), dma((4,))],
         compiler_params=pltpu.CompilerParams(vmem_limit_bytes=VMEM_GRADS),
     )(mixed, tok, down_grad, grad)
 
@@ -656,8 +703,8 @@
         out_shape=[
             pltpu.VMEM((rows, feats), narrow),
             pltpu.VMEM((feats // 2, all_rows), narrow),
-            pltpu.VMEM((hid // 2, feats), narrow),
-            pltpu.VMEM((2, 2, 2, 2, blocks, rows, quarter), narrow),
+            pltpu.VMEM((2, quarter, feats), narrow),
+            pltpu.VMEM((2, 2, 2, blocks, rows, 2 * quarter), narrow),
         ],
         in_specs=[pl.BlockSpec(memory_space=pl.ANY)] * 5,
         out_specs=[pl.BlockSpec(memory_space=pltpu.VMEM)] * 4,
@@ -685,9 +732,10 @@
             dma((2, blocks)),
             dma((2,)),
             dma((units, 3)),
-            dma((units, 2, 2)),
-            dma((units,)),
+            dma((units - 1, 2, 2)),
+            dma((2, 4)),
             dma((units + 1,)),
+            dma((units + 3,)),
             dma((blocks,)),
             dma((blocks,)),
         ],

time: 81.7 us -> 80.4 us (0.984)
  Pallas kernels: 80.9 us -> 79.6 us
    pallas_call x1, Pallas kernels: 74.7 us -> 73.6 us  [grid_device(): pl.pallas_call(functools.partial(exchange_kernel, n_row, n_col), out_shap...]
where the time goes in v4:
time: 80.4 us; the launch traced here: 80.3 us
  Pallas kernels  79.6 us (99%)
    pallas_call x1, Pallas kernels, grid_device(): pl.pallas_call(functools.partial(exchange_kernel, n_row, n_col), out_shap...  73.6 us
    pallas_call x1, Pallas kernels, gradients(): pl.pallas_call(gradient_kernel, out_shape=[jax.ShapeDtypeStruct(mixed.sha...  6.05 us

profile of v4, /device:TPU:0, one launch (start us, length us, event | category | flops | bytes accessed | tf_op | source)
XLA Modules:
  0.0 80.3 jit_solution(5171193460961040240)
XLA Ops:
  0.6 73.6 %shard_map.84 = (bf16[64,1024]{1,0:T(8,128)(2,1)S(1)}, bf16[512,512]{1,0:T(8,128)(2,1)S(1)}, bf16[2,896,1024]{2,1,0:T(8,128)(2,1)S(1)}, bf16[2,2,2,4,64,1792]{5,4,3,2,1,0:T(8,128)(2,1)S(1)}) custom-call(bf16[64,1024]{1,0:T(8,128)(2,1)} %tok_in.1, bf16[1024,3584]{1,0:T(8,128)(2,1)} %gate_in.1, bf16[1024,3584]{1,0:T(8,128)(2,1)} %up_in.1, ...), custom_call_target="tpu_custom_call" | custom-call | tf_op jit(solution)/shard_map/pallas_call | solution.py:701
  74.2 6.1 %shard_map.85 = (bf16[64,1024]{1,0:T(8,128)(2,1)}, bf16[512,3584]{1,0:T(8,128)(2,1)}, bf16[512,3584]{1,0:T(8,128)(2,1)}, bf16[1792,1024]{1,0:T(8,128)(2,1)}) custom-call(bf16[64,1024]{1,0:T(8,128)(2,1)S(1)} %get-tuple-element.8.mix_v, bf16[512,512]{1,0:T(8,128)(2,1)S(1)} %get-tuple-element.9.tok_turned, ...), custom_call_target="tpu_custom_call" | custom-call | tf_op jit(solution)/shard_map/pallas_call | solution.py:677

commit v5 on v4

--- a/solution.py
+++ b/solution.py
@@ -221,7 +221,11 @@
 
     def core_copy(u, a):
         return remote(
-            core_send_v.at[u, a], core_recv_v.at[u, a], sent.at[0], core_recv.at[u, a], core_id
+            core_send_v.at[u, a],
+            core_recv_v.at[u, a],
+            sent.at[0],
+            core_recv.at[u, (a + 1) // 2],
+            core_id,
         )
 
     def product(u, array, side):
@@ -275,13 +279,13 @@
         return remote(x_send_v.at[u, a, span], x_recv_v.at[u, a, span], sent.at[7], recv, x_id)
 
     def x_sem(u, a, part):
-        return x_recv.at[u, a // 2, part]
+        return x_recv.at[u, part]
 
     def x_last_sem(a, part):
         return x_last.at[a // 2, part]
 
-    def x_pair_arrival(u, span, recv):
-        ref = x_recv_v.at[u, 0:2, span]
+    def x_arrival(u, count, span, recv):
+        ref = x_recv_v.at[u, 0:count, span]
         return remote(ref, ref, sent.at[7], recv, x_id)
 
     def near_copy(u, span):
@@ -302,7 +306,7 @@
         return remote(
             grad_v.at[q, :, 0, b, span, core_lanes],
             grad_v.at[q, :, 1, b, span, core_lanes],
-            sent.at[10],
+            sent.at[8],
             y_recv.at[slot],
             y_id,
         )
@@ -310,7 +314,7 @@
     def y_arrival(u, span, slot):
         second, q, b = place(u)
         ref = grad_v.at[1 - q, :, 1, b, span, core_lanes]
-        return remote(ref, ref, sent.at[10], y_recv.at[slot], y_id)
+        return remote(ref, ref, sent.at[8], y_recv.at[slot], y_id)
 
     def yh_copy(b, span):
         return remote(
@@ -331,12 +335,12 @@
         return remote(ref, ref, sent.at[13], late.at[4], core_id)
 
     def mix_copy(b):
-        return remote(mix_send_v.at[b], mix_recv_v.at[b], sent.at[14], mix_recv.at[b], z_ids[b])
+        return remote(mix_send_v.at[b], mix_recv_v.at[b], sent.at[10], mix_recv.at[b], z_ids[b])
 
     def mix_last_copy(half):
         span = part_rows(half, halves)
         return remote(
-            mix_send_v.at[1, span], mix_recv_v.at[1, span], sent.at[14], mix_recv.at[half], z_ids[1]
+            mix_send_v.at[1, span], mix_recv_v.at[1, span], sent.at[10], mix_recv.at[half], z_ids[1]
         )
 
     def all_sent(ref, slot):
@@ -357,7 +361,11 @@
         own_v[u, array] = product(u, array, core)
 
     def finish(u, array):
-        core_copy(u, array).wait_recv()
+        if array == 0:
+            core_copy(u, 0).wait_recv()
+        elif array == 1:
+            ref = core_recv_v.at[u, 1:3]
+            remote(ref, ref, sent.at[0], core_recv.at[u, 1], core_id).wait_recv()
         total = own_v[u, array] + f32(core_recv_v[u, array])
         own_v[u, array] = total
         x_send_v[u, array] = bf16(total)
@@ -442,7 +450,7 @@
     def activate(u, part, parts, recv, slot):
         second, q, b = place(u)
         span = part_rows(part, parts)
-        x_pair_arrival(u, span, recv).wait_recv()
+        x_arrival(u, 2 if parts == pieces else 3, span, recv).wait_recv()
 
         def body(lines):
             gate_sum = own_v[u, 0, lines, :] + f32(x_recv_v[u, 0, lines, :])
@@ -463,7 +471,8 @@
     def factors(u, part, parts, recv, slot):
         second, q, b = place(u)
         span = part_rows(part, parts)
-        x_copy(u, 2, span, recv).wait_recv()
+        if parts == pieces:
+            x_copy(u, 2, span, recv).wait_recv()
 
         def body(lines):
             hidden_grad = own_v[u, 2, lines, :] + f32(x_recv_v[u, 2, lines, :])
@@ -620,13 +629,12 @@
     all_sent(tok_far.at[1:blocks], 5)
     all_sent(cot_v.at[1, 1:blocks], 6)
     all_sent(x_send_v, 7)
-    all_sent(grad_v.at[:, :, 0, :, :, core_lanes], 8)
+    all_sent(grad_v.at[:, :, :, :, :, core_lanes], 8)
     all_sent(hid_v.at[core, 0:2], 9)
-    all_sent(grad_v.at[:, :, 0, :, :, core_lanes], 10)
     all_sent(hid_v.at[core, 2], 11)
     all_sent(grad_v.at[:, :, 1, :, :, core_lanes], 12)
     all_sent(hid_v.at[core, 1], 13)
-    all_sent(mix_send_v.at[1:blocks], 14)
+    all_sent(mix_send_v.at[1:blocks], 10)
 
 
 def gradient_kernel(
@@ -727,12 +735,12 @@
             pltpu.VMEM((blocks, rows, feats), narrow),
             dma((2,)),
             dma((7,)),
-            dma((15,)),
+            dma((14,)),
             dma((5,)),
             dma((2, blocks)),
             dma((2,)),
-            dma((units, 3)),
-            dma((units - 1, 2, 2)),
+            dma((units, 2)),
+            dma((units - 1, 2)),
             dma((2, 4)),
             dma((units + 1,)),
             dma((units + 3,)),

time: 80.4 us -> 80.6 us (level)
  no operation moved by 1% of the time
where the time goes in v5:
time: 80.6 us; the launch traced here: 80.5 us
  Pallas kernels  79.8 us (99%)
    pallas_call x1, Pallas kernels, grid_device(): pl.pallas_call(functools.partial(exchange_kernel, n_row, n_col), out_shap...  73.8 us
    pallas_call x1, Pallas kernels, gradients(): pl.pallas_call(gradient_kernel, out_shape=[jax.ShapeDtypeStruct(mixed.sha...  6.06 us

profile of v5, /device:TPU:0, one launch (start us, length us, event | category | flops | bytes accessed | tf_op | source)
XLA Modules:
  0.0 80.5 jit_solution(12824313603110665525)
XLA Ops:
  0.6 73.8 %shard_map.84 = (bf16[64,1024]{1,0:T(8,128)(2,1)S(1)}, bf16[512,512]{1,0:T(8,128)(2,1)S(1)}, bf16[2,896,1024]{2,1,0:T(8,128)(2,1)S(1)}, bf16[2,2,2,4,64,1792]{5,4,3,2,1,0:T(8,128)(2,1)S(1)}) custom-call(bf16[64,1024]{1,0:T(8,128)(2,1)} %tok_in.1, bf16[1024,3584]{1,0:T(8,128)(2,1)} %gate_in.1, bf16[1024,3584]{1,0:T(8,128)(2,1)} %up_in.1, ...), custom_call_target="tpu_custom_call" | custom-call | tf_op jit(solution)/shard_map/pallas_call | solution.py:709
  74.4 6.1 %shard_map.85 = (bf16[64,1024]{1,0:T(8,128)(2,1)}, bf16[512,3584]{1,0:T(8,128)(2,1)}, bf16[512,3584]{1,0:T(8,128)(2,1)}, bf16[1792,1024]{1,0:T(8,128)(2,1)}) custom-call(bf16[64,1024]{1,0:T(8,128)(2,1)S(1)} %get-tuple-element.8.mix_v, bf16[512,512]{1,0:T(8,128)(2,1)S(1)} %get-tuple-element.9.tok_turned, ...), custom_call_target="tpu_custom_call" | custom-call | tf_op jit(solution)/shard_map/pallas_call | solution.py:685
